TPU v7x, 8 devices: a whole 2x2x1 slice. The times are simulated.
8 devices in a mesh: dp: 1 (over z), t: 2 (over y), stage: 4 (over x, core).
Axes of the slice: x: 2, y: 2, z: 1, core: 2. Of those that a mesh axis runs over, the one named last changes fastest.
Arguments:
- hidden: bfloat16 [4, 24, 1536, 2048], P(('dp', 'stage'))
- w_query: bfloat16 [2048, 3072], P(None, 't')
- w_dkv: bfloat16 [2048, 576], replicated
- latent_gain: bfloat16 [512], replicated
- w_uk: bfloat16 [512, 2048], P(None, 't')
- w_uv: bfloat16 [512, 2048], P(None, 't')
- w_out: bfloat16 [2048, 2048], P('t')
Outputs:
- output 1: bfloat16 [4, 24, 1536, 2048], P(('dp', 'stage'))
- output 2: bfloat16 [4, 24, 1536, 576], P(('dp', 'stage'), 't')
All inputs are finite; a program needn't handle non-finite values.
Results may differ from a plain program's by a relative error of at most 0.00897654.
Values are sent between devices in bfloat16 or wider.
A program may use at most 1.5 GiB of HBM per device.

v0:
```python
import jax
import jax.numpy as jnp
from jax import lax
from jax.sharding import PartitionSpec as P

NOPE_DIM = 128
ROPE_DIM = 64
V_DIM = 128
NORM_EPS = 1e-6
ROPE_BASE = 10000.0


def rope_tables(seq_len):
    half_dim = ROPE_DIM // 2
    positions = jnp.arange(seq_len, dtype=jnp.float32)
    inv_freq = ROPE_BASE ** (-jnp.arange(half_dim, dtype=jnp.float32) / half_dim)
    angles = positions[:, None] * inv_freq[None, :]
    return jnp.cos(angles), jnp.sin(angles)


def apply_rope(vecs, cos_tab, sin_tab):
    half_dim = vecs.shape[-1] // 2
    as_f32 = vecs.astype(jnp.float32)
    low_half = as_f32[..., :half_dim]
    high_half = as_f32[..., half_dim:]
    rotated = jnp.concatenate([low_half * cos_tab - high_half * sin_tab, high_half * cos_tab + low_half * sin_tab], axis=-1)
    return rotated.astype(jnp.bfloat16)


def latent_rows(tokens, w_dkv, latent_gain, cos_tab, sin_tab):
    kv_rank = latent_gain.shape[0]
    compressed = jnp.einsum("bsd,dc->bsc", tokens, w_dkv, preferred_element_type=jnp.float32).astype(jnp.bfloat16)
    c_raw = compressed[..., :kv_rank].astype(jnp.float32)
    inv_rms = lax.rsqrt(jnp.mean(c_raw * c_raw, axis=-1, keepdims=True) + NORM_EPS)
    c_kv = (c_raw * inv_rms * latent_gain.astype(jnp.float32)).astype(jnp.bfloat16)
    k_rope = apply_rope(compressed[..., kv_rank:], cos_tab, sin_tab)
    return jnp.concatenate([c_kv, k_rope], axis=-1)


def causal_heads(q_nope, q_rope, k_nope, k_rope, values):
    seq_len = q_nope.shape[1]
    n_blocks = max(1, min(8, seq_len // 128))
    block_len = seq_len // n_blocks
    score_scale = (q_nope.shape[-1] + q_rope.shape[-1]) ** -0.5
    pieces = []
    for block_idx in range(n_blocks):
        start_row = block_idx * block_len
        stop_row = start_row + block_len
        scores = jnp.einsum("bqhe,bkhe->bhqk", q_nope[:, start_row:stop_row], k_nope[:, :stop_row], preferred_element_type=jnp.float32)
        scores = scores + jnp.einsum("bqhe,bke->bhqk", q_rope[:, start_row:stop_row], k_rope[:, :stop_row], preferred_element_type=jnp.float32)
        q_pos = start_row + jnp.arange(block_len)[:, None]
        k_pos = jnp.arange(stop_row)[None, :]
        scores = jnp.where(k_pos <= q_pos, scores * score_scale, -jnp.inf)
        row_peak = jnp.max(scores, axis=-1, keepdims=True)
        weights = jnp.exp(scores - row_peak)
        row_total = jnp.sum(weights, axis=-1)
        mixed = jnp.einsum("bhqk,bkhe->bqhe", weights.astype(jnp.bfloat16), values[:, :stop_row], preferred_element_type=jnp.float32)
        pieces.append((mixed / jnp.transpose(row_total, (0, 2, 1))[..., None]).astype(jnp.bfloat16))
    return jnp.concatenate(pieces, axis=1)


def attention_partial(tokens, latent, w_query, w_uk, w_uv, w_out, cos_tab, sin_tab):
    kv_rank = w_uk.shape[0]
    batch, seq_len = tokens.shape[0], tokens.shape[1]
    heads_here = w_uk.shape[1] // NOPE_DIM
    queries = jnp.einsum("bsd,dn->bsn", tokens, w_query, preferred_element_type=jnp.float32).astype(jnp.bfloat16)
    queries = queries.reshape(batch, seq_len, heads_here, NOPE_DIM + ROPE_DIM)
    q_rope = apply_rope(queries[..., NOPE_DIM:], cos_tab[:, None, :], sin_tab[:, None, :])
    k_nope = jnp.einsum("bsr,rn->bsn", latent[..., :kv_rank], w_uk, preferred_element_type=jnp.float32).astype(jnp.bfloat16)
    k_nope = k_nope.reshape(batch, seq_len, heads_here, NOPE_DIM)
    values = jnp.einsum("bsr,rn->bsn", latent[..., :kv_rank], w_uv, preferred_element_type=jnp.float32).astype(jnp.bfloat16)
    values = values.reshape(batch, seq_len, heads_here, V_DIM)
    head_mix = causal_heads(queries[..., :NOPE_DIM], q_rope, k_nope, latent[..., kv_rank:], values)
    head_mix = head_mix.reshape(batch, seq_len, heads_here * V_DIM)
    return jnp.einsum("bsn,nd->bsd", head_mix, w_out, preferred_element_type=jnp.float32)


def solution(mesh):
    n_tp = mesh.shape["t"]
    half_stage = mesh.shape["stage"] // 2
    hand_pairs = [(source_idx, source_idx + half_stage) for source_idx in range(half_stage)]
    slot_spec = P(("dp", "stage"), None, None, None)
    cache_spec = P(("dp", "stage"), "t", None, None)

    def device_step(hidden, w_query, w_dkv, latent_gain, w_uk, w_uv, w_out):
        tokens = hidden[0]
        local_rows = tokens.shape[0] // n_tp
        t_index = lax.axis_index("t")
        cos_tab, sin_tab = rope_tables(tokens.shape[1])
        my_tokens = lax.dynamic_slice_in_dim(tokens, t_index * local_rows, local_rows, axis=0)
        my_latent = latent_rows(my_tokens, w_dkv, latent_gain, cos_tab, sin_tab)
        all_latent = lax.all_gather(my_latent, "t", axis=0, tiled=True)
        handed = lax.ppermute(my_latent, "stage", hand_pairs)
        part_sum = attention_partial(tokens, all_latent, w_query, w_uk, w_uv, w_out, cos_tab, sin_tab)
        summed = lax.psum(part_sum.astype(jnp.bfloat16), "t")
        is_prompt = lax.axis_index("stage") < half_stage
        out_rows = jnp.where(is_prompt, summed, jnp.zeros_like(summed))
        return out_rows[None], handed[None]

    return jax.shard_map(device_step, mesh=mesh, in_specs=(slot_spec, P(None, "t"), P(None, None), P(None), P(None, "t"), P(None, "t"), P("t", None)), out_specs=(slot_spec, cache_spec), check_vma=False)
```

profile of v0, /device:TPU:0, one launch (start us, length us, event | category | flops | bytes accessed | tf_op | source)
XLA Modules:
  0.0 6362.2 jit_solution(1736441211518397566)
XLA Ops:
  8.8 51.5 fusion.78
  71.5 18.2 fusion.63
  90.4 17.2 pad_maximum_fusion
  114.4 248.3 %fusion.23 = bf16[24,1536,1536]{1,2,0:T(8,128)(2,1)} fusion(bf16[1,24,1536,2048]{3,2,1,0:T(8,128)(2,1)} %param.7, bf16[2048,1536]{1,0:T(8,128)(2,1)} %param.8), kind=kOutput, calls=%fused_computation.34 | convolution fusion | flops 231984857088 | bytes 270532608 | tf_op jit(solution)/shard_map/bsd,dn->bsn/dot_general | solution.py:66
  362.7 36.1 slice_convert_fusion
  398.8 39.5 add_convert_fusion
  438.3 160.3 %all-gather.2.cloned.1.call-done = bf16[24,1536,576]{1,2,0:T(8,128)(2,1)} async-done(((bf16[12,1536,576]{1,2,0:T(8,128)(2,1)}), bf16[24,1536,576]{1,2,0:T(8,128)(2,1)}) %all-gather.2.cloned.1.call-update) | async-done | bytes 42467344 | tf_op jit(solution)/shard_map/all_gather | solution.py:92
  598.6 49.6 convolution_convert_fusion.1
  648.2 21.3 fusion.101
  669.5 46.5 fusion.73
  716.0 68.5 %fusion.54 = f32[24,8,192,960]{3,2,1,0:T(8,128)} fusion(bf16[24,1536,8,128]{1,3,2,0:T(8,128)(2,1)} %bitcast.8, bf16[24,1536,8,192]{1,3,2,0:T(8,128)(2,1)} %bitcast.6), kind=kOutput, calls=%fused_computation.79 | convolution fusion | flops 9059696640 | bytes 204472320 | tf_op jit(solution)/shard_map/bqhe,bkhe->bhqk/dot_general | solution.py:49
  784.5 26.6 fusion.179
  811.1 16.6 fusion.68
  827.8 49.6 convolution_convert_fusion.2
  877.4 22.9 fusion.105
  900.3 24.4 fusion.149
  924.7 50.0 fusion.180
  974.7 18.4 fusion.56
  993.1 28.9 fusion.106
  1022.0 64.9 %fusion.181 = (f32[24,8,192]{2,1,0:T(8,128)S(1)}, f32[24,8,192,576]{3,2,1,0:T(8,128)}) fusion(f32[24,8,192,576]{3,2,1,0:T(8,128)} %fusion.73, bf16[24,1536,8,32]{1,3,2,0:T(8,128)(2,1)} %get-tuple-element.3, bf16[24,1536,8,32]{1,3,2,0:T(8,128)(2,1)} %get-tuple-element.2, bf16[24,1536,576]{1,2,0:T(8,128)(2,1)} %all-gather.2.cloned.1.call-done, ...), kind=kOutput, calls=%fused_computation.210 | convolution fusion | flops 2812243968 | bytes 219279360 | tf_op jit(solution)/shard_map/bqhe,bke->bhqk/dot_general | solution.py:50
  1086.9 29.4 fusion.36
  1116.4 43.5 fusion.107
  1159.9 44.4 fusion.154
  1204.3 89.6 %fusion.182 = (f32[24,8,192]{2,1,0:T(8,128)S(1)}, f32[24,8,192,768]{3,2,1,0:T(8,128)}) fusion(f32[24,768,192,8]{1,2,3,0:T(8,128)} %fusion.154, bf16[24,1536,8,128]{1,3,2,0:T(8,128)(2,1)} %bitcast.8, bf16[24,1536,8,192]{1,3,2,0:T(8,128)(2,1)} %bitcast.6, pred[192,768]{1,0:T(8,128)(4,1)S(1)} %copy-done.6), kind=kOutput, calls=%fused_computation.211 | convolution fusion | flops 7360966656 | bytes 277118976 | tf_op jit(solution)/shard_map/bqhe,bkhe->bhqk/dot_general | solution.py:49
  1293.9 34.7 fusion.29
  1328.6 50.9 fusion.108
  1379.5 101.4 %fusion.183 = (f32[24,8,192]{2,1,0:T(8,128)S(1)}, f32[24,8,192,960]{3,2,1,0:T(8,128)}) fusion(f32[24,8,192,960]{3,2,1,0:T(8,128)} %fusion.54, bf16[24,1536,8,32]{1,3,2,0:T(8,128)(2,1)} %get-tuple-element.3, bf16[24,1536,8,32]{1,3,2,0:T(8,128)(2,1)} %get-tuple-element.2, bf16[24,1536,576]{1,2,0:T(8,128)(2,1)} %all-gather.2.cloned.1.call-done, ...), kind=kOutput, calls=%fused_computation.212 | convolution fusion | flops 4680806400 | bytes 333778944 | tf_op jit(solution)/shard_map/bqhe,bke->bhqk/dot_general | solution.py:50
  1480.9 45.5 fusion.16
  1526.4 65.2 %fusion.109 = bf16[24,1536,8,128]{3,1,2,0:T(8,128)(2,1)} fusion(bf16[24,1536,8,128]{3,1,2,0:T(8,128)(2,1)} %fusion.108, f32[24,192,8]{1,2,0:T(8,128)S(1)} %bitcast.225, bf16[24,1536,8,128]{1,3,2,0:T(8,128)(2,1)} %bitcast.3, f32[24,8,192,960]{3,2,1,0:T(8,128)} %get-tuple-element.17, f32[24,8,192]{2,1,0:T(8,128)S(1)} %get-tuple-element.16), kind=kOutput, calls=%fused_computation.145 | convolution fusion | flops 9139912704 | bytes 211058688 | tf_op jit(solution)/shard_map/bhqk,bkhe->bqhe/dot_general | solution.py:57
  1591.6 60.1 fusion.159
  1651.7 133.0 %fusion.184 = (f32[24,8,192]{2,1,0:T(8,128)S(1)}, f32[24,8,192,1152]{3,2,1,0:T(8,128)}) fusion(f32[24,1152,192,8]{1,2,3,0:T(8,128)} %fusion.159, bf16[24,1536,8,128]{1,3,2,0:T(8,128)(2,1)} %bitcast.8, bf16[24,1536,8,192]{1,3,2,0:T(8,128)(2,1)} %bitcast.6, pred[192,1152]{1,0:T(8,128)(4,1)S(1)} %copy-done.4), kind=kOutput, calls=%fused_computation.213 | convolution fusion | flops 11041468416 | bytes 409313280 | tf_op jit(solution)/shard_map/bqhe,bkhe->bhqk/dot_general | solution.py:49
  1784.7 51.4 fusion.14
  1836.0 72.4 %fusion.110 = bf16[24,1536,8,128]{3,1,2,0:T(8,128)(2,1)} fusion(bf16[24,1536,8,128]{3,1,2,0:T(8,128)(2,1)} %fusion.109, f32[24,192,8]{1,2,0:T(8,128)S(1)} %bitcast.222, bf16[24,1536,8,128]{1,3,2,0:T(8,128)(2,1)} %bitcast.3, f32[24,8,192,1152]{3,2,1,0:T(8,128)} %get-tuple-element.19, f32[24,8,192]{2,1,0:T(8,128)S(1)} %get-tuple-element.18), kind=kOutput, calls=%fused_computation.146 | convolution fusion | flops 10966007808 | bytes 236224512 | tf_op jit(solution)/shard_map/bhqk,bkhe->bqhe/dot_general | solution.py:57
  1908.5 71.3 %fusion.144 = f32[24,1344,192,8]{1,2,3,0:T(8,128)} fusion(bf16[24,1536,8,32]{1,3,2,0:T(8,128)(2,1)} %get-tuple-element.3, bf16[24,1536,8,32]{1,3,2,0:T(8,128)(2,1)} %get-tuple-element.2, bf16[24,1536,576]{1,2,0:T(8,128)(2,1)} %all-gather.2.cloned.1.call-done), kind=kOutput, calls=%fused_computation.150 | convolution fusion | flops 6351224832 | bytes 240254976 | tf_op jit(solution)/shard_map/bqhe,bke->bhqk/dot_general | solution.py:50
  1979.8 170.4 %fusion.185 = (f32[24,8,192]{2,1,0:T(8,128)S(1)}, f32[24,8,192,1344]{3,2,1,0:T(8,128)}) fusion(f32[24,1344,192,8]{1,2,3,0:T(8,128)} %fusion.144, bf16[24,1536,8,128]{1,3,2,0:T(8,128)(2,1)} %bitcast.8, bf16[24,1536,8,192]{1,3,2,0:T(8,128)(2,1)} %bitcast.6, pred[192,1344]{1,0:T(8,128)(4,1)S(1)} %copy-done.3), kind=kOutput, calls=%fused_computation.214 | convolution fusion | flops 12881719296 | bytes 487993344 | tf_op jit(solution)/shard_map/bqhe,bkhe->bhqk/dot_general | solution.py:49
  2150.2 62.6 fusion.6
  2212.8 86.5 %fusion.111 = bf16[24,1536,8,128]{3,1,2,0:T(8,128)(2,1)} fusion(bf16[24,1536,8,128]{3,1,2,0:T(8,128)(2,1)} %fusion.110, f32[24,192,8]{1,2,0:T(8,128)S(1)} %bitcast.223, bf16[24,1536,8,128]{1,3,2,0:T(8,128)(2,1)} %bitcast.3, f32[24,8,192,1344]{3,2,1,0:T(8,128)} %get-tuple-element.21, f32[24,8,192]{2,1,0:T(8,128)S(1)} %get-tuple-element.20), kind=kOutput, calls=%fused_computation.147 | convolution fusion | flops 12792102912 | bytes 286556160 | tf_op jit(solution)/shard_map/bhqk,bkhe->bqhe/dot_general | solution.py:57
  2299.4 80.7 %fusion.161 = f32[24,1536,192,8]{1,2,3,0:T(8,128)} fusion(bf16[24,1536,8,32]{1,3,2,0:T(8,128)(2,1)} %get-tuple-element.2, bf16[24,1536,8,32]{1,3,2,0:T(8,128)(2,1)} %get-tuple-element.3, bf16[24,1536,576]{1,2,0:T(8,128)(2,1)} %all-gather.2.cloned.1.call-done), kind=kOutput, calls=%fused_computation.161 | convolution fusion | flops 7257194496 | bytes 268959744 | tf_op jit(solution)/shard_map/bqhe,bke->bhqk/dot_general | solution.py:50
  2380.1 177.5 %fusion.186 = (f32[24,8,192]{2,1,0:T(8,128)S(1)}, f32[24,8,192,1536]{3,2,1,0:T(8,128)}) fusion(f32[24,1536,192,8]{1,2,3,0:T(8,128)} %fusion.161, bf16[24,1536,8,128]{1,3,2,0:T(8,128)(2,1)} %bitcast.8, bf16[24,1536,8,192]{1,3,2,0:T(8,128)(2,1)} %bitcast.6, pred[192,1536]{1,0:T(8,128)(4,1)S(1)} %copy-done.2), kind=kOutput, calls=%fused_computation.215 | convolution fusion | flops 14721970176 | bytes 541507584 | tf_op jit(solution)/shard_map/bqhe,bkhe->bhqk/dot_general | solution.py:49
  2557.6 68.1 %fusion.4 = f32[24,8,192]{2,1,0:T(8,128)S(1)} fusion(f32[24,8,192,1536]{3,2,1,0:T(8,128)} %get-tuple-element.23, f32[24,8,192]{2,1,0:T(8,128)S(1)} %get-tuple-element.22), kind=kLoop, calls=%fused_computation.8 | loop fusion | flops 113209344 | bytes 226787328 | tf_op jit(solution)/shard_map/reduce_sum | solution.py:56
  2625.7 94.8 %fusion.112 = bf16[24,1536,8,128]{3,1,2,0:T(8,128)(2,1)} fusion(bf16[24,1536,8,128]{3,1,2,0:T(8,128)(2,1)} %fusion.111, f32[24,192,8]{1,2,0:T(8,128)S(1)} %bitcast.226, bf16[24,1536,8,128]{1,3,2,0:T(8,128)(2,1)} %bitcast.3, f32[24,8,192,1536]{3,2,1,0:T(8,128)} %get-tuple-element.23, f32[24,8,192]{2,1,0:T(8,128)S(1)} %get-tuple-element.22), kind=kOutput, calls=%fused_computation.148 | convolution fusion | flops 14618198016 | bytes 311721984 | tf_op jit(solution)/shard_map/bhqk,bkhe->bqhe/dot_general | solution.py:57
  2720.5 96.7 %copy.100 = bf16[24,1536,8,128]{1,3,2,0:T(8,128)(2,1)} copy(bf16[24,1536,8,128]{3,1,2,0:T(8,128)(2,1)} %fusion.112) | data formatting | bytes 150994944 | tf_op jit(solution)/shard_map/concatenate | solution.py:59
  2817.1 168.3 %convolution_convert_fusion = bf16[24,1536,2048]{2,1,0:T(8,128)(2,1)} fusion(bf16[24,1536,1024]{1,2,0:T(8,128)(2,1)} %bitcast.49, bf16[1024,2048]{1,0:T(8,128)(2,1)} %param.13), kind=kOutput, calls=%fused_computation.33 | convolution fusion | flops 154694320128 | bytes 230686720 | tf_op jit(solution)/shard_map/bsn,nd->bsd/dot_general | solution.py:75
  2985.4 10.6 collective-permute-start
  2996.0 447.5 %collective-permute-done = bf16[12,1536,576]{1,2,0:T(8,128)(2,1)} collective-permute-done((bf16[12,1536,576]{1,2,0:T(8,128)(2,1)}, bf16[12,1536,576]{1,2,0:T(8,128)(2,1)}, u32[]{:S(2)}, u32[]{:S(2)}) %collective-permute-start) | collective-permute-done | bytes 21233696 | tf_op jit(solution)/shard_map/ppermute | solution.py:93
  3443.5 2797.9 %all-reduce.2.cloned.1.call-done = bf16[24,1536,2048]{2,1,0:T(8,128)(2,1)} async-done(((bf16[24,1536,2048]{2,1,0:T(8,128)(2,1)}), bf16[24,1536,2048]{2,1,0:T(8,128)(2,1)}) %all-reduce.2.cloned.1.call-update) | async-done | bytes 150994960 | tf_op jit(solution)/shard_map/psum | solution.py:95
  6241.4 98.6 %select_bitcast_fusion = bf16[1,24,1536,2048]{3,2,1,0:T(8,128)(2,1)} fusion(bf16[24,1536,2048]{2,1,0:T(8,128)(2,1)} %all-reduce.2.cloned.1.call-done, pred[]{:T(512)S(6)} %lt.6), kind=kLoop, calls=%fused_computation.21 | loop fusion | flops 75497472 | bytes 301989888 | tf_op jit(solution)/shard_map/broadcast_in_dim | solution.py:98
  6339.9 15.0 copy.152
  (60 shorter events, 20.2 us)
Async XLA Ops:
  7.2 1.7 copy-start
  7.2 591.4 %all-gather.2.cloned.1.call-start = ((), (), s32[]{:S(2)}) async-start(), calls=%async_computation | async-start | bytes 63700992 | tf_op jit(solution)/shard_map/all_gather | solution.py:92
  8.8 62.5 copy-start.14
  71.4 19.0 copy-start.9
  71.4 19.0 copy-start.11
  107.7 6133.7 %all-reduce.2.cloned.1.call-start = ((), (), s32[]{:S(2)}) async-start(), calls=%async_computation.1 | async-start | bytes 301989888 | tf_op jit(solution)/shard_map/psum | solution.py:95
  362.6 36.1 copy-start.10
  362.7 36.1 copy-start.12
  398.8 199.8 %copy-start.15 = (bf16[512,1024]{1,0:T(8,128)(2,1)S(1)}, bf16[512,1024]{1,0:T(8,128)(2,1)}, u32[]{:S(2)}) copy-start(bf16[512,1024]{1,0:T(8,128)(2,1)} %param.11) | copy-start | bytes 3145732
  716.0 68.5 %copy-start.13 = (pred[192,192]{0,1:T(8,128)(4,1)S(1)}, pred[192,192]{0,1:T(8,128)(4,1)}, u32[]{:S(2)}) copy-start(pred[192,192]{0,1:T(8,128)(4,1)} %iota_compare_fusion.7) | copy-start | bytes 110596
  784.5 43.2 copy-start.16
  900.3 24.4 copy-start.8
  993.1 28.9 copy-start.7
  1159.9 44.5 copy-start.6
  1328.6 50.9 copy-start.5
  1591.6 60.1 copy-start.4
  1908.5 71.3 %copy-start.3 = (pred[192,1344]{1,0:T(8,128)(4,1)S(1)}, pred[192,1344]{1,0:T(8,128)(4,1)}, u32[]{:S(2)}) copy-start(pred[192,1344]{1,0:T(8,128)(4,1)} %iota_compare_fusion.1) | copy-start | bytes 774148
  2299.4 80.7 %copy-start.2 = (pred[192,1536]{1,0:T(8,128)(4,1)S(1)}, pred[192,1536]{1,0:T(8,128)(4,1)}, u32[]{:S(2)}) copy-start(pred[192,1536]{1,0:T(8,128)(4,1)} %iota_compare_fusion) | copy-start | bytes 884740
  2985.4 458.1 %collective-permute-start = (bf16[12,1536,576]{1,2,0:T(8,128)(2,1)}, bf16[12,1536,576]{1,2,0:T(8,128)(2,1)}, u32[]{:S(2)}, u32[]{:S(2)}) collective-permute-start(bf16[12,1536,576]{1,2,0:T(8,128)(2,1)} %pad_maximum_fusion), channel_id=1, source_target_pairs={{0,2},{1,3},{4,6},{5,7}} | collective-permute-start | bytes 63701000 | tf_op jit(solution)/shard_map/ppermute | solution.py:93
  6241.4 113.6 %copy-start.1 = (bf16[2048,576]{0,1:T(8,128)(2,1)S(1)}, bf16[2048,576]{0,1:T(8,128)(2,1)}, u32[]{:S(2)}) copy-start(bf16[2048,576]{0,1:T(8,128)(2,1)} %param.9) | copy-start | bytes 7077892
Sparse Core Ops, SparseCore 0:
  107.8 490.7 all-gather.1
  2985.5 3255.7 all-reduce.1
where the time goes:
time: 6370 us; the launch traced here: 6360 us
  waiting for transfers between devices  3410 us (54%)
  matrix products  2260 us (35%)
  other arithmetic  555 us (9%)
  local copies, waits for them, and re-layouts  113 us (2%)
    psum x1, waiting for transfers between devices, device_step(): summed = lax.psum(part_sum.astype(jnp.bfloat16), 't')  2800 us
    dot_general x8, matrix products, causal_heads(): jnp.einsum('bqhe,bkhe->bhqk', q_nope[:, start_row:stop_row], k_nope[:, :s...  757 us
    dot_general x8, matrix products, causal_heads(): jnp.einsum('bqhe,bke->bhqk', q_rope[:, start_row:stop_row], k_rope[:, :st...  474 us
    dot_general x8, matrix products, causal_heads(): jnp.einsum('bhqk,bkhe->bqhe', weights.astype(jnp.bfloat16), values[:, :st...  465 us
    ppermute x1, waiting for transfers between devices, device_step(): handed = lax.ppermute(my_latent, 'stage', hand_pairs)  448 us
    reduce_sum x8, other arithmetic, causal_heads(): row_total = jnp.sum(weights, axis=-1)  327 us
    dot_general x1, matrix products, attention_partial(): jnp.einsum('bsd,dn->bsn', tokens, w_query, preferred_element_type=jnp.flo...  248 us
    dot_general x1, matrix products, attention_partial(): jnp.einsum('bsn,nd->bsd', head_mix, w_out, preferred_element_type=jnp.flo...  168 us
  transfers between devices with their start and end apart: 3, of which 3 were waited for; matrix products, arithmetic and copies ran while one was open for 5% of the time, Pallas kernels for 0%

commit v1 on v0

v1 whole, which is shorter than its diff:
```python
import functools
import math

import jax
import jax.numpy as jnp
from jax import lax
from jax.experimental import pallas as pl
from jax.experimental.layout import Layout, with_layout_constraint
from jax.experimental.pallas import tpu as pltpu
from jax.sharding import PartitionSpec as P


NOPE_DIM = 128
ROPE_DIM = 64
HALF_ROPE = ROPE_DIM // 2
NORM_EPS = 1e-6
ROPE_BASE = 10000.0
BLOCK = 256
LANES = 128


N_FAR = 7
N_SWAP = 1
STEP_CALLS = (1, 1, 1, 1, 1, 1, 1)
TAIL_CALLS = (1, 1)


def rope_tables(seq_len):
    positions = jnp.arange(seq_len, dtype=jnp.float32)
    inv_freq = ROPE_BASE ** (-jnp.arange(HALF_ROPE, dtype=jnp.float32) / HALF_ROPE)
    angles = positions[:, None] * inv_freq[None, :]
    cos_tab, sin_tab = jnp.cos(angles), jnp.sin(angles)
    reps = LANES // ROPE_DIM
    return jnp.tile(cos_tab, (1, 2 * reps)), jnp.tile(jnp.concatenate([-sin_tab, sin_tab], axis=1), (1, reps))


def attend_kernel(n_ret, aliased, ids, flags, hid, recv, w_dkv, gain, wq_own, wq_oth, kvo_own, kvo_oth, cos_ref, sin_ref, *rest):
    if aliased:
        rest = rest[1:]
    if n_ret:
        out_ref, lat_ref, ret_ref, *scratch = rest
    else:
        out_ref, lat_ref, *scratch = rest
        ret_ref = None
    x_s, k_s, v_s, kr_s, q_s, qr_s, o_s, s0_s, s1_s, p0_s, p1_s, t0_s, t1_s = scratch
    req, blk = pl.program_id(0), pl.program_id(1)
    n_blocks = k_s.shape[0] // BLOCK
    kv_rank = gain.shape[1]
    half = kvo_own.shape[1] // 2
    n_heads = k_s.shape[1] // NOPE_DIM
    is_far = flags[0] == 1
    active = flags[1 + req] == 1
    scale = (NOPE_DIM + ROPE_DIM) ** -0.5 * math.log2(math.e)

    def rope(vecs):
        lane = lax.broadcasted_iota(jnp.int32, (BLOCK, LANES), 1)
        low = lane % ROPE_DIM < HALF_ROPE
        cos_tab, sin_tab = cos_ref[...], sin_ref[...]
        parts = []
        for start in range(0, vecs.shape[1], LANES):
            vec = vecs[:, start:start + LANES].astype(jnp.float32)
            other = jnp.where(low, pltpu.roll(vec, LANES - HALF_ROPE, 1), pltpu.roll(vec, HALF_ROPE, 1))
            parts.append((vec * cos_tab + other * sin_tab).astype(jnp.bfloat16))
        return jnp.concatenate(parts, axis=1)

    @pl.when(active)
    def _():
        @pl.when(is_far)
        def _():
            x_s[...] = recv[0]

        @pl.when(jnp.logical_not(is_far))
        def _():
            x_s[...] = hid[0]

        rows = pl.ds(pl.multiple_of(blk * BLOCK, BLOCK), BLOCK)
        comp = jnp.dot(x_s[...], w_dkv[...], preferred_element_type=jnp.float32).astype(jnp.bfloat16)
        raw = comp[:, :kv_rank].astype(jnp.float32)
        inv_rms = lax.rsqrt(jnp.mean(raw * raw, axis=-1, keepdims=True) + NORM_EPS)
        c_kv = (raw * inv_rms * gain[...]).astype(jnp.bfloat16)
        k_rope = rope(comp[:, kv_rank:])
        kr_s[rows, :] = k_rope
        lat_ref[0, :, :kv_rank] = c_kv
        lat_ref[0, :, kv_rank:] = k_rope[:, :ROPE_DIM]
        for idx, (wq, kvo) in enumerate(((wq_own, kvo_own), (wq_oth, kvo_oth))):
            cols = slice(idx * half, (idx + 1) * half)
            k_s[rows, cols] = jnp.dot(c_kv, kvo[:kv_rank, :half], preferred_element_type=jnp.float32).astype(jnp.bfloat16)
            v_s[rows, cols] = jnp.dot(c_kv, kvo[:kv_rank, half:], preferred_element_type=jnp.float32).astype(jnp.bfloat16)
            q_s[:, cols] = jnp.dot(x_s[...], wq[:, :half], preferred_element_type=jnp.float32).astype(jnp.bfloat16)
            q_rope = jnp.dot(x_s[...], wq[:, half:], preferred_element_type=jnp.float32).astype(jnp.bfloat16)
            qr_s[:, idx * half // 2:(idx + 1) * half // 2] = rope(q_rope)

        for step in range(n_blocks):
            @pl.when(blk == step)
            def _(step=step):
                prev = step * BLOCK
                length = prev + BLOCK
                causal = lax.broadcasted_iota(jnp.int32, (BLOCK, BLOCK), 1) <= lax.broadcasted_iota(jnp.int32, (BLOCK, BLOCK), 0)

                def score(head, odd, dst):
                    cols = pl.ds(pl.multiple_of(head * NOPE_DIM, NOPE_DIM), NOPE_DIM)
                    thin = pl.ds(pl.multiple_of(head // 2 * LANES, LANES), LANES)
                    query = jnp.concatenate([q_s[:, cols], qr_s[:, thin]], axis=1)
                    keys = jnp.concatenate([k_s[:length, cols], kr_s[:length, odd * LANES:(odd + 1) * LANES]], axis=1)
                    dst[:, :length] = lax.dot_general(query, keys, (((1,), (1,)), ((), ())), preferred_element_type=jnp.float32)

                def weigh(src, dst, total_ref):
                    diag = jnp.where(causal, src[:, prev:length], -jnp.inf)
                    peak = jnp.max(diag, axis=-1, keepdims=True)
                    if prev:
                        peak = jnp.maximum(peak, jnp.max(src[:, :prev], axis=-1, keepdims=True))
                    e_diag = jnp.exp2((diag - peak) * scale)
                    total = jnp.sum(e_diag, axis=-1, keepdims=True)
                    dst[:, prev:length] = e_diag.astype(jnp.bfloat16)
                    if prev:
                        e_past = jnp.exp2((src[:, :prev] - peak) * scale)
                        total = total + jnp.sum(e_past, axis=-1, keepdims=True)
                        dst[:, :prev] = e_past.astype(jnp.bfloat16)
                    total_ref[...] = jnp.broadcast_to(total, total_ref.shape)

                def mix(head, src, total_ref):
                    cols = pl.ds(pl.multiple_of(head * NOPE_DIM, NOPE_DIM), NOPE_DIM)
                    mixed = jnp.dot(src[:, :length], v_s[:length, cols], preferred_element_type=jnp.float32)
                    o_s[:, cols] = (mixed / total_ref[...]).astype(jnp.bfloat16)

                def pair(idx, carry):
                    head = idx * 2
                    score(head + 1, 1, s1_s)
                    weigh(s0_s, p0_s, t0_s)
                    mix(jnp.maximum(head - 1, 0), p1_s, t1_s)
                    score(jnp.minimum(head + 2, n_heads - 2), 0, s0_s)
                    weigh(s1_s, p1_s, t1_s)
                    mix(head, p0_s, t0_s)
                    return carry

                score(0, 0, s0_s)
                lax.fori_loop(0, n_heads // 2, pair, 0)
                mix(n_heads - 1, p1_s, t1_s)

        y = jnp.dot(o_s[:, :half], kvo_own[kv_rank:, :], preferred_element_type=jnp.float32)
        y = y + jnp.dot(o_s[:, half:], kvo_oth[kv_rank:, :], preferred_element_type=jnp.float32)
        y = y.astype(jnp.bfloat16)
        if ret_ref is not None:
            @pl.when(req < n_ret)
            def _():
                ret_ref[0] = y

        @pl.when(jnp.logical_not(is_far))
        def _():
            out_ref[0] = y

    @pl.when(jnp.logical_not(jnp.logical_and(active, jnp.logical_not(is_far))))
    def _():
        out_ref[0] = jnp.zeros(out_ref.shape[1:], out_ref.dtype)


def attend(ids, flags, hidden, recv, weights, out_prev, n_ret):
    n_req = ids.shape[0]
    _, seq_len, width = hidden.shape
    w_dkv, gain, wq_own, wq_oth, kvo_own, kvo_oth, _, _ = weights
    n_blocks = seq_len // BLOCK
    kv_rank = gain.shape[1]
    half = kvo_own.shape[1] // 2
    lat_width = kv_rank + ROPE_DIM
    whole = lambda arr: pl.BlockSpec(arr.shape, lambda r, i, ids, flags: (0, 0), pipeline_mode=pl.Buffered(1))
    in_specs = [
        pl.BlockSpec((1, BLOCK, width), lambda r, i, ids, flags: (jnp.where(flags[0] == 1, 0, ids[r]), jnp.where(flags[0] == 1, 0, i), 0)),
        pl.BlockSpec((1, BLOCK, width), lambda r, i, ids, flags: (0, jnp.where((flags[0] == 1) & (r == 0), i, 0), 0)),
        *[whole(arr) for arr in (w_dkv, gain, wq_own, wq_oth, kvo_own, kvo_oth)],
        pl.BlockSpec((BLOCK, LANES), lambda r, i, ids, flags: (i, 0)),
        pl.BlockSpec((BLOCK, LANES), lambda r, i, ids, flags: (i, 0)),
    ]
    args = [hidden, recv, *weights]
    out_shape = [jax.ShapeDtypeStruct(hidden.shape, jnp.bfloat16), jax.ShapeDtypeStruct((n_req, seq_len, lat_width), jnp.bfloat16)]
    out_specs = [
        pl.BlockSpec((1, BLOCK, width), lambda r, i, ids, flags: (ids[r], i, 0)),
        pl.BlockSpec((1, BLOCK, lat_width), lambda r, i, ids, flags: (r, i, 0)),
    ]
    if n_ret:
        out_shape.append(jax.ShapeDtypeStruct((n_ret, seq_len, width), jnp.bfloat16))
        out_specs.append(pl.BlockSpec((1, BLOCK, width), lambda r, i, ids, flags: (jnp.minimum(r, n_ret - 1), jnp.where(r < n_ret, i, n_blocks - 1), 0)))
    aliases = {}
    if out_prev is not None:
        in_specs.append(pl.BlockSpec(memory_space=pl.ANY))
        args.append(out_prev)
        aliases = {2 + len(args) - 1: 0}
    flops = n_req * seq_len * (2 * width * (768 + 3 * half * 2 // 2 * 1 + 2 * half) + 8 * kv_rank * half + 2 * half * seq_len * 3)
    outs = pl.pallas_call(
        functools.partial(attend_kernel, n_ret, out_prev is not None),
        out_shape=out_shape,
        grid_spec=pltpu.PrefetchScalarGridSpec(
            num_scalar_prefetch=2,
            grid=(n_req, n_blocks),
            in_specs=in_specs,
            out_specs=out_specs,
            scratch_shapes=[
                pltpu.VMEM((BLOCK, width), jnp.bfloat16),
                pltpu.VMEM((seq_len, 2 * half), jnp.bfloat16),
                pltpu.VMEM((seq_len, 2 * half), jnp.bfloat16),
                pltpu.VMEM((seq_len, 2 * LANES), jnp.bfloat16),
                pltpu.VMEM((BLOCK, 2 * half), jnp.bfloat16),
                pltpu.VMEM((BLOCK, half), jnp.bfloat16),
                pltpu.VMEM((BLOCK, 2 * half), jnp.bfloat16),
                *[pltpu.VMEM((BLOCK, seq_len), jnp.float32)] * 2,
                *[pltpu.VMEM((BLOCK, seq_len), jnp.bfloat16)] * 2,
                *[pltpu.VMEM((BLOCK, NOPE_DIM), jnp.float32)] * 2,
            ],
        ),
        input_output_aliases=aliases,
        compiler_params=pltpu.CompilerParams(dimension_semantics=("arbitrary", "arbitrary"), vmem_limit_bytes=66_000_000),
        cost_estimate=pl.CostEstimate(flops=flops, bytes_accessed=n_req * seq_len * width * 6, transcendentals=n_req * seq_len * seq_len * 8),
        name="attend",
    )(ids, flags, *args)
    return outs if n_ret else (*outs, None)


def solution(mesh):
    n_stage = mesh.shape["stage"]
    half_stage = n_stage // 2
    down = [(idx, idx + half_stage) for idx in range(half_stage)]
    up = [(idx + half_stage, idx) for idx in range(half_stage)]
    cores = [(idx, idx ^ 1) for idx in range(n_stage)]
    swap = [(0, 1), (1, 0)]
    slot_spec = P(("dp", "stage"), None, None, None)
    cache_spec = P(("dp", "stage"), "t", None, None)

    def other_half(arr, core):
        rows = arr.shape[0] // 2
        mine = lax.ppermute(lax.dynamic_slice_in_dim(arr, core * rows, rows, axis=0), "t", swap)
        theirs = lax.ppermute(mine, "stage", cores)
        first = jnp.where(core == 0, mine, theirs)
        second = jnp.where(core == 0, theirs, mine)
        return jnp.concatenate([first, second], axis=0)

    def device_step(hidden, w_query, w_dkv, latent_gain, w_uk, w_uv, w_out):
        tokens = hidden[0]
        n_all, seq_len, width = tokens.shape
        kv_rank = latent_gain.shape[0]
        n_half = n_all // 2
        t_index = lax.axis_index("t")
        stage = lax.axis_index("stage")
        is_prompt = stage < half_stage
        core = stage % 2
        own, oth = t_index * n_half, (1 - t_index) * n_half

        arrivals = []
        for idx in range(N_FAR):
            index = own + idx
            if arrivals:
                index, _ = lax.optimization_barrier((index, arrivals[-1]))
            piece = lax.dynamic_slice_in_dim(tokens, index, 1, axis=0)
            arrivals.append(lax.ppermute(piece, "stage", down))

        heads_here = w_uk.shape[1] // NOPE_DIM
        wq = w_query.reshape(width, heads_here, NOPE_DIM + ROPE_DIM)
        wq_own = jnp.concatenate([wq[:, :, :NOPE_DIM].reshape(width, -1), wq[:, :, NOPE_DIM:].reshape(width, -1)], axis=1)
        kvo_own = jnp.concatenate([jnp.concatenate([w_uk, w_uv], axis=1), w_out], axis=0)
        wq_oth, kvo_oth = other_half(wq_own, core), other_half(kvo_own, core)
        blank = jnp.zeros((width, ROPE_DIM), w_dkv.dtype)
        w_dkv_wide = jnp.concatenate([w_dkv, blank, blank, w_dkv[:, kv_rank:]], axis=1)
        gain = latent_gain.astype(jnp.float32)[None, :]
        weights = (w_dkv_wide, gain, wq_own, wq_oth, kvo_own, kvo_oth, *rope_tables(seq_len))

        ids = jnp.concatenate([own + jnp.arange(N_FAR, n_half), oth + jnp.arange(N_FAR + N_SWAP, n_half)]).astype(jnp.int32)
        far = jnp.where(is_prompt, 0, 1).astype(jnp.int32)
        place = lambda out, block, index: lax.dynamic_update_slice(out, jnp.where(is_prompt, block, jnp.zeros_like(block)), (index, 0, 0))

        out, done = None, 0
        latents, far_latents = [], []
        backs, movements = {}, {}

        def put(idx, source):
            nonlocal out
            for block, index in source.pop(idx, ()):
                out = place(out, block, index)

        def run(count, recv, n_ret, far_active):
            nonlocal out, done
            flags = jnp.stack([far, *[jnp.where(is_prompt, 1, 1 if far_active and idx == 0 else 0).astype(jnp.int32) for idx in range(count)]])
            out, lat, ret = attend(ids[done:done + count], flags, tokens, recv, weights, out, n_ret)
            n_send = max(0, min(count, n_half - N_FAR - done))
            if n_send:
                sent, _ = lax.optimization_barrier((lat[:n_send], arrivals[-1]))
                latents.append(lax.ppermute(sent, "stage", down))
            if far_active:
                far_latents.append(lat[:1])
            done += count
            return ret

        n_steps = len(STEP_CALLS)
        for idx, count in enumerate(STEP_CALLS):
            put(idx - 2, backs)
            put(idx - 4, movements)
            ret = run(count, arrivals[idx], 1, True)
            if idx < N_SWAP:
                swapped = lax.ppermute(ret, "t", swap)
            back = lax.ppermute(ret, "stage", up)
            moved = lax.ppermute(back, "t", swap)
            backs[idx] = [(back, own + idx)]
            movements[idx] = [(moved, oth + idx)]
            if idx < N_SWAP:
                movements[idx].append((swapped, oth + N_FAR + idx))
        for idx, count in enumerate(TAIL_CALLS):
            put(n_steps + idx - 2, backs)
            put(n_steps + idx - 4, movements)
            run(count, tokens, 0, False)
        for idx in range(n_steps):
            put(idx, backs)
            put(idx, movements)
        pieces = [*far_latents, *latents]

        def empty(parts):
            return with_layout_constraint(jnp.zeros((n_half, kv_rank + ROPE_DIM, seq_len), jnp.bfloat16), Layout((0, 1, 2)))

        def gathered(parts):
            return with_layout_constraint(jnp.swapaxes(jnp.concatenate(parts, axis=0), 1, 2), Layout((0, 1, 2)))

        latent = jnp.swapaxes(lax.cond(is_prompt, empty, gathered, pieces), 1, 2)
        return out[None], latent[None]

    in_specs = (slot_spec, P(None, "t"), P(None, None), P(None), P(None, "t"), P(None, "t"), P("t", None))
    return jax.shard_map(device_step, mesh=mesh, in_specs=in_specs, out_specs=(slot_spec, cache_spec), check_vma=False)
```

time: 6370 us -> 1620 us (0.25)
  waiting for transfers between devices: 3410 us -> 236 us
  matrix products: 2260 us -> 0 us
  Pallas kernels: 0 us -> 1020 us
  other arithmetic: 555 us -> 157 us
  starting transfers between devices: 10.6 us -> 82.1 us
    psum x1 -> x0, waiting for transfers between devices: 2800 us -> none  [device_step(): summed = lax.psum(part_sum.astype(jnp.bfloat16), 't')]
    dot_general x29 -> x0, matrix products: 2260 us -> none  [the longest x8 757 us: causal_heads(): jnp.einsum('bqhe,bkhe->bhqk', q_nope[:, start_row:stop_row], k_nope[:, :s...]
    pallas_call x0 -> x9, Pallas kernels: none -> 1020 us  [attend(): pl.pallas_call(functools.partial(attend_kernel, n_ret, out_prev is not No...]
    reduce_sum x9 -> x0, other arithmetic: 335 us -> none  [the longest x8 327 us: causal_heads(): row_total = jnp.sum(weights, axis=-1)]
    ppermute x1 -> x31, waiting for transfers between devices: 448 us -> 236 us  [the longest x7 122 us: device_step(): moved = lax.ppermute(back, 't', swap)]
    all_gather x1 -> x0, waiting for transfers between devices: 160 us -> none  [device_step(): all_latent = lax.all_gather(my_latent, 't', axis=0, tiled=True)]
    dynamic_update_slice x0 -> x15, other arithmetic: none -> 116 us  [device_step(): lax.dynamic_update_slice(out, jnp.where(is_prompt, block, jnp.zeros_like(...]
    broadcast_in_dim x1, other arithmetic: 98.6 us -> 0.58 us  [device_step(): gain = latent_gain.astype(jnp.float32)[None, :]]
  transfers between devices with their start and end apart: 3 -> 31, of which waited for: 3 -> 8; matrix products, arithmetic and copies ran while one was open for 5% -> 16% of each run, Pallas kernels for 0% -> 63%
where the time goes in v1:
time: 1620 us; the launch traced here: 1610 us
  Pallas kernels  1020 us (63%)
  waiting for transfers between devices  236 us (15%)
  other arithmetic  157 us (10%)
  local copies, waits for them, and re-layouts  111 us (7%)
  starting transfers between devices  82.1 us (5%)
    pallas_call x9, Pallas kernels, attend(): pl.pallas_call(functools.partial(attend_kernel, n_ret, out_prev is not No...  1020 us
    ppermute x7, waiting for transfers between devices, device_step(): moved = lax.ppermute(back, 't', swap)  122 us
    dynamic_update_slice x15, other arithmetic, device_step(): lax.dynamic_update_slice(out, jnp.where(is_prompt, block, jnp.zeros_like(...  116 us
    ppermute x2, waiting for transfers between devices, other_half(): lax.ppermute(lax.dynamic_slice_in_dim(arr, core * rows, rows, axis=0), 't...  93.6 us
    dynamic_slice x7, local copies, waits for them, and re-layouts, device_step(): piece = lax.dynamic_slice_in_dim(tokens, index, 1, axis=0)  46.4 us
    ppermute x7, starting transfers between devices, device_step(): arrivals.append(lax.ppermute(piece, 'stage', down))  43.9 us
  transfers between devices with their start and end apart: 31, of which 8 were waited for; matrix products, arithmetic and copies ran while one was open for 16% of the time, Pallas kernels for 63%

profile of v1, /device:TPU:0, one launch (start us, length us, event | category | flops | bytes accessed | tf_op | source)
XLA Modules:
  0.0 1605.7 jit_solution(4152838539297561955)
XLA Ops:
  0.7 6.8 dynamic-slice_bitcast_fusion.6
  7.4 7.9 collective-permute-start.4
  15.3 14.4 pad_maximum_fusion.2.kvo_own
  36.1 8.6 copy.68
  44.7 4.8 slice.49
  52.7 6.4 copy.101
  66.0 39.9 %collective-permute-done.2 = bf16[768,2048]{1,0:T(8,128)(2,1)} collective-permute-done((bf16[768,2048]{1,0:T(8,128)(2,1)}, bf16[768,2048]{1,0:T(8,128)(2,1)}, u32[]{:S(2)}, u32[]{:S(2)}) %collective-permute-start.2) | collective-permute-done | bytes 3145760 | tf_op jit(solution)/shard_map/ppermute | solution.py:229
  118.1 53.7 %collective-permute-done = bf16[1024,1536]{1,0:T(8,128)(2,1)} collective-permute-done((bf16[1024,1536]{1,0:T(8,128)(2,1)}, bf16[1024,1536]{1,0:T(8,128)(2,1)}, u32[]{:S(2)}, u32[]{:S(2)}) %collective-permute-start) | collective-permute-done | bytes 3145760 | tf_op jit(solution)/shard_map/ppermute | solution.py:229
  179.2 6.6 dynamic-slice_bitcast_fusion.5
  203.1 112.8 %attend.9 = (bf16[24,1536,2048]{2,1,0:T(8,128)(2,1)}, bf16[1,1536,576]{2,1,0:T(8,128)(2,1)}, bf16[1,1536,2048]{2,1,0:T(8,128)(2,1)}) custom-call(s32[1]{0:T(128)} %get-tuple-element.149.ids, s32[2]{0:T(128)} %pad_add_fusion.1.flags, bf16[24,1536,2048]{2,1,0:T(8,128)(2,1)} %bitcast.3.hid.recv, bf16[1,1536,2048]{2,1,0:T(8,128)(2,1)} %collective-permute-done.4.recv, ...), custom_call_target="tpu_custom_call" | custom-call | flops 57982058496 | bytes 18874368 | tf_op jit(solution)/shard_map/attend/pallas_call | solution.py:188
  323.2 6.6 dynamic-slice_bitcast_fusion.4
  329.8 7.0 collective-permute-start.6
  336.8 113.3 %attend.10 = (bf16[24,1536,2048]{2,1,0:T(8,128)(2,1)}, bf16[1,1536,576]{2,1,0:T(8,128)(2,1)}, bf16[1,1536,2048]{2,1,0:T(8,128)(2,1)}) custom-call(s32[1]{0:T(128)} %get-tuple-element.150.ids, s32[2]{0:T(128)} %pad_add_fusion.1.flags, bf16[24,1536,2048]{2,1,0:T(8,128)(2,1)} %bitcast.3.hid.recv, ...), custom_call_target="tpu_custom_call", output_to_operand_aliasing={{0}: (12, {})} | custom-call | flops 57982058496 | bytes 18874368 | tf_op jit(solution)/shard_map/attend/pallas_call | solution.py:188
  451.3 5.2 collective-permute-done.11
  458.1 7.7 select_dynamic-update-slice_fusion.12.rest_0_
  469.3 6.6 dynamic-slice_bitcast_fusion.3
  475.9 7.0 collective-permute-start.7
  483.0 113.1 %attend.11 = (bf16[24,1536,2048]{2,1,0:T(8,128)(2,1)}, bf16[1,1536,576]{2,1,0:T(8,128)(2,1)}, bf16[1,1536,2048]{2,1,0:T(8,128)(2,1)}) custom-call(s32[1]{0:T(128)} %get-tuple-element.151.ids, s32[2]{0:T(128)} %pad_add_fusion.1.flags, bf16[24,1536,2048]{2,1,0:T(8,128)(2,1)} %bitcast.3.hid.recv, ...), custom_call_target="tpu_custom_call", output_to_operand_aliasing={{0}: (12, {})} | custom-call | flops 57982058496 | bytes 18874368 | tf_op jit(solution)/shard_map/attend/pallas_call | solution.py:188
  598.9 7.7 select_dynamic-update-slice_fusion.11.rest_0_
  606.7 8.0 collective-permute-done.7.recv
  614.6 6.6 dynamic-slice_bitcast_fusion.2
  621.2 7.0 collective-permute-start.8
  628.2 112.9 %attend.12 = (bf16[24,1536,2048]{2,1,0:T(8,128)(2,1)}, bf16[1,1536,576]{2,1,0:T(8,128)(2,1)}, bf16[1,1536,2048]{2,1,0:T(8,128)(2,1)}) custom-call(s32[1]{0:T(128)} %get-tuple-element.152.ids, s32[2]{0:T(128)} %pad_add_fusion.1.flags, bf16[24,1536,2048]{2,1,0:T(8,128)(2,1)} %bitcast.3.hid.recv, ...), custom_call_target="tpu_custom_call", output_to_operand_aliasing={{0}: (12, {})} | custom-call | flops 57982058496 | bytes 18874368 | tf_op jit(solution)/shard_map/attend/pallas_call | solution.py:188
  742.4 7.7 select_dynamic-update-slice_fusion.10
  751.6 7.7 select_dynamic-update-slice_fusion.9
  759.3 7.7 select_dynamic-update-slice_fusion.8.rest_0_
  767.0 6.6 dynamic-slice_bitcast_fusion.1
  777.6 113.3 %attend.13 = (bf16[24,1536,2048]{2,1,0:T(8,128)(2,1)}, bf16[1,1536,576]{2,1,0:T(8,128)(2,1)}, bf16[1,1536,2048]{2,1,0:T(8,128)(2,1)}) custom-call(s32[1]{0:T(128)} %get-tuple-element.153.ids, s32[2]{0:T(128)} %pad_add_fusion.1.flags, bf16[24,1536,2048]{2,1,0:T(8,128)(2,1)} %bitcast.3.hid.recv, ...), custom_call_target="tpu_custom_call", output_to_operand_aliasing={{0}: (12, {})} | custom-call | flops 57982058496 | bytes 18874368 | tf_op jit(solution)/shard_map/attend/pallas_call | solution.py:188
  892.7 7.7 select_dynamic-update-slice_fusion.7
  900.5 7.7 select_dynamic-update-slice_fusion.6.rest_0_
  908.2 6.6 dynamic-slice_bitcast_fusion
  914.8 7.1 collective-permute-start.10
  921.9 113.1 %attend.14 = (bf16[24,1536,2048]{2,1,0:T(8,128)(2,1)}, bf16[1,1536,576]{2,1,0:T(8,128)(2,1)}, bf16[1,1536,2048]{2,1,0:T(8,128)(2,1)}) custom-call(s32[1]{0:T(128)} %get-tuple-element.154.ids, s32[2]{0:T(128)} %pad_add_fusion.1.flags, bf16[24,1536,2048]{2,1,0:T(8,128)(2,1)} %bitcast.3.hid.recv, ...), custom_call_target="tpu_custom_call", output_to_operand_aliasing={{0}: (12, {})} | custom-call | flops 57982058496 | bytes 18874368 | tf_op jit(solution)/shard_map/attend/pallas_call | solution.py:188
  1036.8 7.7 select_dynamic-update-slice_fusion.5
  1044.5 7.7 select_dynamic-update-slice_fusion.4.rest_0_
  1069.6 113.3 %attend.15 = (bf16[24,1536,2048]{2,1,0:T(8,128)(2,1)}, bf16[1,1536,576]{2,1,0:T(8,128)(2,1)}, bf16[1,1536,2048]{2,1,0:T(8,128)(2,1)}) custom-call(s32[1]{0:T(128)} %get-tuple-element.155.ids, s32[2]{0:T(128)} %pad_add_fusion.1.flags, bf16[24,1536,2048]{2,1,0:T(8,128)(2,1)} %bitcast.3.hid.recv, ...), custom_call_target="tpu_custom_call", output_to_operand_aliasing={{0}: (12, {})} | custom-call | flops 57982058496 | bytes 18874368 | tf_op jit(solution)/shard_map/attend/pallas_call | solution.py:188
  1185.4 7.8 select_dynamic-update-slice_fusion.3
  1200.8 7.7 select_dynamic-update-slice_fusion.2.rest_0_
  1208.5 5.6 collective-permute-start.27
  1216.6 113.0 %attend.16 = (bf16[24,1536,2048]{2,1,0:T(8,128)(2,1)}, bf16[1,1536,576]{2,1,0:T(8,128)(2,1)}) custom-call(s32[1]{0:T(128)} %get-tuple-element.156.ids, s32[2]{0:T(128)} %pad_add_fusion.flags, bf16[24,1536,2048]{2,1,0:T(8,128)(2,1)} %bitcast.3.hid.recv, bf16[24,1536,2048]{2,1,0:T(8,128)(2,1)} %bitcast.3.hid.recv, ...), custom_call_target="tpu_custom_call", output_to_operand_aliasing={{0}: (12, {})} | custom-call | flops 57982058496 | bytes 18874368 | tf_op jit(solution)/shard_map/attend/pallas_call | solution.py:188
  1330.2 7.4 conditional.1
  1330.2 7.4 broadcast.37
  1339.1 7.7 select_dynamic-update-slice_fusion.1
  1346.8 7.7 select_dynamic-update-slice_fusion.rest_0_
  1354.5 113.3 %attend.17 = (bf16[24,1536,2048]{2,1,0:T(8,128)(2,1)}, bf16[1,1536,576]{2,1,0:T(8,128)(2,1)}) custom-call(s32[1]{0:T(128)} %get-tuple-element.157.ids, s32[2]{0:T(128)} %pad_add_fusion.flags, bf16[24,1536,2048]{2,1,0:T(8,128)(2,1)} %bitcast.3.hid.recv, bf16[24,1536,2048]{2,1,0:T(8,128)(2,1)} %bitcast.3.hid.recv, ...), custom_call_target="tpu_custom_call", output_to_operand_aliasing={{0}: (12, {})} | custom-call | flops 57982058496 | bytes 18874368 | tf_op jit(solution)/shard_map/attend/pallas_call | solution.py:188
  1468.3 7.7 bitcast_dynamic-update-slice_fusion.1
  1476.0 121.6 %collective-permute-done.25 = bf16[1,1536,2048]{2,1,0:T(8,128)(2,1)} collective-permute-done((bf16[1,1536,2048]{2,1,0:T(8,128)(2,1)}, bf16[1,1536,2048]{2,1,0:T(8,128)(2,1)}, u32[]{:S(2)}, u32[]{:S(2)}) %collective-permute-start.25) | collective-permute-done | bytes 6291488 | tf_op jit(solution)/shard_map/ppermute | solution.py:298
  1597.6 7.7 bitcast_dynamic-update-slice_fusion
  (98 shorter events, 112.7 us)
Async XLA Ops:
  0.6 14.7 copy-start.6
  0.6 14.7 copy-start.7
  7.4 171.8 %collective-permute-start.4 = (bf16[1,1536,2048]{2,1,0:T(8,128)(2,1)}, bf16[1,1536,2048]{2,1,0:T(8,128)(2,1)}, u32[]{:S(2)}, u32[]{:S(2)}) collective-permute-start(bf16[1,1536,2048]{2,1,0:T(8,128)(2,1)} %dynamic-slice_bitcast_fusion.6), channel_id=1, source_target_pairs={{0,2},{1,3},{4,6},{5,7}} | collective-permute-start | bytes 18874376 | tf_op jit(solution)/shard_map/ppermute | solution.py:252
  29.7 2.7 copy-start
  34.5 71.3 %collective-permute-start.2 = (bf16[768,2048]{1,0:T(8,128)(2,1)}, bf16[768,2048]{1,0:T(8,128)(2,1)}, u32[]{:S(2)}, u32[]{:S(2)}) collective-permute-start(bf16[768,2048]{1,0:T(8,128)(2,1)} %constant_dynamic-slice_fusion), channel_id=1, source_target_pairs={{0,4},{4,0},{1,5},{5,1},{2,6},{6,2},{3,7},{7,3}} | collective-permute-start | bytes 9437192 | tf_op jit(solution)/shard_map/ppermute | solution.py:229
  65.5 106.4 %collective-permute-start = (bf16[1024,1536]{1,0:T(8,128)(2,1)}, bf16[1024,1536]{1,0:T(8,128)(2,1)}, u32[]{:S(2)}, u32[]{:S(2)}) collective-permute-start(bf16[1024,1536]{1,0:T(8,128)(2,1)} %fusion), channel_id=1, source_target_pairs={{0,4},{4,0},{1,5},{5,1},{2,6},{6,2},{3,7},{7,3}} | collective-permute-start | bytes 9437192 | tf_op jit(solution)/shard_map/ppermute | solution.py:229
  105.8 83.9 %collective-permute-start.3 = (bf16[768,2048]{1,0:T(8,128)(2,1)}, bf16[768,2048]{1,0:T(8,128)(2,1)}, u32[]{:S(2)}, u32[]{:S(2)}) collective-permute-start(bf16[768,2048]{1,0:T(8,128)(2,1)} %collective-permute-done.2), channel_id=1, source_target_pairs={{0,1},{1,0},{2,3},{3,2},{4,5},{5,4},{6,7},{7,6}} | collective-permute-start | bytes 9437192 | tf_op jit(solution)/shard_map/ppermute | solution.py:230
  105.8 10.4 copy-start.8
  116.9 59.0 %copy-start.1 = (bf16[2048,1024]{1,0:T(8,128)(2,1)S(1)}, bf16[2048,1024]{1,0:T(8,128)(2,1)}, u32[]{:S(2)}) copy-start(bf16[2048,1024]{1,0:T(8,128)(2,1)} %copy.101) | copy-start | bytes 12582916
  171.8 24.9 %collective-permute-start.1 = (bf16[1024,1536]{1,0:T(8,128)(2,1)}, bf16[1024,1536]{1,0:T(8,128)(2,1)}, u32[]{:S(2)}, u32[]{:S(2)}) collective-permute-start(bf16[1024,1536]{1,0:T(8,128)(2,1)} %collective-permute-done), channel_id=1, source_target_pairs={{0,1},{1,0},{2,3},{3,2},{4,5},{5,4},{6,7},{7,6}} | collective-permute-start | bytes 9437192 | tf_op jit(solution)/shard_map/ppermute | solution.py:230
  185.9 137.3 %collective-permute-start.5 = (bf16[1,1536,2048]{2,1,0:T(8,128)(2,1)}, bf16[1,1536,2048]{2,1,0:T(8,128)(2,1)}, u32[]{:S(2)}, u32[]{:S(2)}) collective-permute-start(bf16[1,1536,2048]{2,1,0:T(8,128)(2,1)} %dynamic-slice_bitcast_fusion.5), channel_id=1, source_target_pairs={{0,2},{1,3},{4,6},{5,7}} | collective-permute-start | bytes 18874376 | tf_op jit(solution)/shard_map/ppermute | solution.py:252
  315.9 140.6 %collective-permute-start.11 = (bf16[1,1536,2048]{2,1,0:T(8,128)(2,1)}, bf16[1,1536,2048]{2,1,0:T(8,128)(2,1)}, u32[]{:S(2)}, u32[]{:S(2)}) collective-permute-start(bf16[1,1536,2048]{2,1,0:T(8,128)(2,1)} %get-tuple-element.83), channel_id=1, source_target_pairs={{2,0},{3,1},{6,4},{7,5}} | collective-permute-start | bytes 18874376 | tf_op jit(solution)/shard_map/ppermute | solution.py:297
  318.5 440.9 %collective-permute-start.15 = (bf16[1,1536,2048]{2,1,0:T(8,128)(2,1)}, bf16[1,1536,2048]{2,1,0:T(8,128)(2,1)}, u32[]{:S(2)}, u32[]{:S(2)}) collective-permute-start(bf16[1,1536,2048]{2,1,0:T(8,128)(2,1)} %get-tuple-element.83), channel_id=1, source_target_pairs={{0,4},{4,0},{1,5},{5,1},{2,6},{6,2},{3,7},{7,3}} | collective-permute-start | bytes 18874376 | tf_op jit(solution)/shard_map/ppermute | solution.py:296
  329.8 139.5 %collective-permute-start.6 = (bf16[1,1536,2048]{2,1,0:T(8,128)(2,1)}, bf16[1,1536,2048]{2,1,0:T(8,128)(2,1)}, u32[]{:S(2)}, u32[]{:S(2)}) collective-permute-start(bf16[1,1536,2048]{2,1,0:T(8,128)(2,1)} %dynamic-slice_bitcast_fusion.4), channel_id=1, source_target_pairs={{0,2},{1,3},{4,6},{5,7}} | collective-permute-start | bytes 18874376 | tf_op jit(solution)/shard_map/ppermute | solution.py:252
  450.0 147.3 %collective-permute-start.12 = (bf16[1,1536,2048]{2,1,0:T(8,128)(2,1)}, bf16[1,1536,2048]{2,1,0:T(8,128)(2,1)}, u32[]{:S(2)}, u32[]{:S(2)}) collective-permute-start(bf16[1,1536,2048]{2,1,0:T(8,128)(2,1)} %get-tuple-element.85), channel_id=1, source_target_pairs={{2,0},{3,1},{6,4},{7,5}} | collective-permute-start | bytes 18874376 | tf_op jit(solution)/shard_map/ppermute | solution.py:297
  456.5 293.6 %collective-permute-start.14 = (bf16[1,1536,2048]{2,1,0:T(8,128)(2,1)}, bf16[1,1536,2048]{2,1,0:T(8,128)(2,1)}, u32[]{:S(2)}, u32[]{:S(2)}) collective-permute-start(bf16[1,1536,2048]{2,1,0:T(8,128)(2,1)} %collective-permute-done.11), channel_id=1, source_target_pairs={{0,4},{4,0},{1,5},{5,1},{2,6},{6,2},{3,7},{7,3}} | collective-permute-start | bytes 18874376 | tf_op jit(solution)/shard_map/ppermute | solution.py:298
  475.9 138.7 %collective-permute-start.7 = (bf16[1,1536,2048]{2,1,0:T(8,128)(2,1)}, bf16[1,1536,2048]{2,1,0:T(8,128)(2,1)}, u32[]{:S(2)}, u32[]{:S(2)}) collective-permute-start(bf16[1,1536,2048]{2,1,0:T(8,128)(2,1)} %dynamic-slice_bitcast_fusion.3), channel_id=1, source_target_pairs={{0,2},{1,3},{4,6},{5,7}} | collective-permute-start | bytes 18874376 | tf_op jit(solution)/shard_map/ppermute | solution.py:252
  596.1 145.0 %collective-permute-start.13 = (bf16[1,1536,2048]{2,1,0:T(8,128)(2,1)}, bf16[1,1536,2048]{2,1,0:T(8,128)(2,1)}, u32[]{:S(2)}, u32[]{:S(2)}) collective-permute-start(bf16[1,1536,2048]{2,1,0:T(8,128)(2,1)} %get-tuple-element.87), channel_id=1, source_target_pairs={{2,0},{3,1},{6,4},{7,5}} | collective-permute-start | bytes 18874376 | tf_op jit(solution)/shard_map/ppermute | solution.py:297
  597.4 303.1 %collective-permute-start.17 = (bf16[1,1536,2048]{2,1,0:T(8,128)(2,1)}, bf16[1,1536,2048]{2,1,0:T(8,128)(2,1)}, u32[]{:S(2)}, u32[]{:S(2)}) collective-permute-start(bf16[1,1536,2048]{2,1,0:T(8,128)(2,1)} %collective-permute-done.12), channel_id=1, source_target_pairs={{0,4},{4,0},{1,5},{5,1},{2,6},{6,2},{3,7},{7,3}} | collective-permute-start | bytes 18874376 | tf_op jit(solution)/shard_map/ppermute | solution.py:298
  621.2 145.8 %collective-permute-start.8 = (bf16[1,1536,2048]{2,1,0:T(8,128)(2,1)}, bf16[1,1536,2048]{2,1,0:T(8,128)(2,1)}, u32[]{:S(2)}, u32[]{:S(2)}) collective-permute-start(bf16[1,1536,2048]{2,1,0:T(8,128)(2,1)} %dynamic-slice_bitcast_fusion.2), channel_id=1, source_target_pairs={{0,2},{1,3},{4,6},{5,7}} | collective-permute-start | bytes 18874376 | tf_op jit(solution)/shard_map/ppermute | solution.py:252
  741.1 151.1 %collective-permute-start.16 = (bf16[1,1536,2048]{2,1,0:T(8,128)(2,1)}, bf16[1,1536,2048]{2,1,0:T(8,128)(2,1)}, u32[]{:S(2)}, u32[]{:S(2)}) collective-permute-start(bf16[1,1536,2048]{2,1,0:T(8,128)(2,1)} %get-tuple-element.89), channel_id=1, source_target_pairs={{2,0},{3,1},{6,4},{7,5}} | collective-permute-start | bytes 18874376 | tf_op jit(solution)/shard_map/ppermute | solution.py:297
  750.1 294.4 %collective-permute-start.19 = (bf16[1,1536,2048]{2,1,0:T(8,128)(2,1)}, bf16[1,1536,2048]{2,1,0:T(8,128)(2,1)}, u32[]{:S(2)}, u32[]{:S(2)}) collective-permute-start(bf16[1,1536,2048]{2,1,0:T(8,128)(2,1)} %collective-permute-done.13), channel_id=1, source_target_pairs={{0,4},{4,0},{1,5},{5,1},{2,6},{6,2},{3,7},{7,3}} | collective-permute-start | bytes 18874376 | tf_op jit(solution)/shard_map/ppermute | solution.py:298
  773.6 134.5 %collective-permute-start.9 = (bf16[1,1536,2048]{2,1,0:T(8,128)(2,1)}, bf16[1,1536,2048]{2,1,0:T(8,128)(2,1)}, u32[]{:S(2)}, u32[]{:S(2)}) collective-permute-start(bf16[1,1536,2048]{2,1,0:T(8,128)(2,1)} %dynamic-slice_bitcast_fusion.1), channel_id=1, source_target_pairs={{0,2},{1,3},{4,6},{5,7}} | collective-permute-start | bytes 18874376 | tf_op jit(solution)/shard_map/ppermute | solution.py:252
  890.9 145.3 %collective-permute-start.18 = (bf16[1,1536,2048]{2,1,0:T(8,128)(2,1)}, bf16[1,1536,2048]{2,1,0:T(8,128)(2,1)}, u32[]{:S(2)}, u32[]{:S(2)}) collective-permute-start(bf16[1,1536,2048]{2,1,0:T(8,128)(2,1)} %get-tuple-element.91), channel_id=1, source_target_pairs={{2,0},{3,1},{6,4},{7,5}} | collective-permute-start | bytes 18874376 | tf_op jit(solution)/shard_map/ppermute | solution.py:297
  892.2 307.3 %collective-permute-start.21 = (bf16[1,1536,2048]{2,1,0:T(8,128)(2,1)}, bf16[1,1536,2048]{2,1,0:T(8,128)(2,1)}, u32[]{:S(2)}, u32[]{:S(2)}) collective-permute-start(bf16[1,1536,2048]{2,1,0:T(8,128)(2,1)} %collective-permute-done.16), channel_id=1, source_target_pairs={{0,4},{4,0},{1,5},{5,1},{2,6},{6,2},{3,7},{7,3}} | collective-permute-start | bytes 18874376 | tf_op jit(solution)/shard_map/ppermute | solution.py:298
  914.8 137.4 %collective-permute-start.10 = (bf16[1,1536,2048]{2,1,0:T(8,128)(2,1)}, bf16[1,1536,2048]{2,1,0:T(8,128)(2,1)}, u32[]{:S(2)}, u32[]{:S(2)}) collective-permute-start(bf16[1,1536,2048]{2,1,0:T(8,128)(2,1)} %dynamic-slice_bitcast_fusion), channel_id=1, source_target_pairs={{0,2},{1,3},{4,6},{5,7}} | collective-permute-start | bytes 18874376 | tf_op jit(solution)/shard_map/ppermute | solution.py:252
  1034.9 148.0 %collective-permute-start.20 = (bf16[1,1536,2048]{2,1,0:T(8,128)(2,1)}, bf16[1,1536,2048]{2,1,0:T(8,128)(2,1)}, u32[]{:S(2)}, u32[]{:S(2)}) collective-permute-start(bf16[1,1536,2048]{2,1,0:T(8,128)(2,1)} %get-tuple-element.93), channel_id=1, source_target_pairs={{2,0},{3,1},{6,4},{7,5}} | collective-permute-start | bytes 18874376 | tf_op jit(solution)/shard_map/ppermute | solution.py:297
  1036.2 310.5 %collective-permute-start.23 = (bf16[1,1536,2048]{2,1,0:T(8,128)(2,1)}, bf16[1,1536,2048]{2,1,0:T(8,128)(2,1)}, u32[]{:S(2)}, u32[]{:S(2)}) collective-permute-start(bf16[1,1536,2048]{2,1,0:T(8,128)(2,1)} %collective-permute-done.18), channel_id=1, source_target_pairs={{0,4},{4,0},{1,5},{5,1},{2,6},{6,2},{3,7},{7,3}} | collective-permute-start | bytes 18874376 | tf_op jit(solution)/shard_map/ppermute | solution.py:298
  1052.2 15.1 copy-start.4
  1056.3 152.2 %collective-permute-start.30 = (bf16[1,1536,576]{1,2,0:T(8,128)(2,1)}, bf16[1,1536,576]{1,2,0:T(8,128)(2,1)}, u32[]{:S(2)}, u32[]{:S(2)}) collective-permute-start(bf16[1,1536,576]{1,2,0:T(8,128)(2,1)} %copy.93), channel_id=1, source_target_pairs={{0,2},{1,3},{4,6},{5,7}} | collective-permute-start | bytes 5308424 | tf_op jit(solution)/shard_map/ppermute | solution.py:284
  1064.8 149.3 %collective-permute-start.29 = (bf16[1,1536,576]{1,2,0:T(8,128)(2,1)}, bf16[1,1536,576]{1,2,0:T(8,128)(2,1)}, u32[]{:S(2)}, u32[]{:S(2)}) collective-permute-start(bf16[1,1536,576]{1,2,0:T(8,128)(2,1)} %copy.92), channel_id=1, source_target_pairs={{0,2},{1,3},{4,6},{5,7}} | collective-permute-start | bytes 5308424 | tf_op jit(solution)/shard_map/ppermute | solution.py:284
  1182.9 146.7 %collective-permute-start.28 = (bf16[1,1536,576]{1,2,0:T(8,128)(2,1)}, bf16[1,1536,576]{1,2,0:T(8,128)(2,1)}, u32[]{:S(2)}, u32[]{:S(2)}) collective-permute-start(bf16[1,1536,576]{1,2,0:T(8,128)(2,1)} %copy.91), channel_id=1, source_target_pairs={{0,2},{1,3},{4,6},{5,7}} | collective-permute-start | bytes 5308424 | tf_op jit(solution)/shard_map/ppermute | solution.py:284
  1185.4 11.8 copy-start.2
  1199.5 138.1 %collective-permute-start.22 = (bf16[1,1536,2048]{2,1,0:T(8,128)(2,1)}, bf16[1,1536,2048]{2,1,0:T(8,128)(2,1)}, u32[]{:S(2)}, u32[]{:S(2)}) collective-permute-start(bf16[1,1536,2048]{2,1,0:T(8,128)(2,1)} %get-tuple-element.95), channel_id=1, source_target_pairs={{2,0},{3,1},{6,4},{7,5}} | collective-permute-start | bytes 18874376 | tf_op jit(solution)/shard_map/ppermute | solution.py:297
  1208.5 121.7 %collective-permute-start.27 = (bf16[1,1536,576]{1,2,0:T(8,128)(2,1)}, bf16[1,1536,576]{1,2,0:T(8,128)(2,1)}, u32[]{:S(2)}, u32[]{:S(2)}) collective-permute-start(bf16[1,1536,576]{1,2,0:T(8,128)(2,1)} %copy.90), channel_id=1, source_target_pairs={{0,2},{1,3},{4,6},{5,7}} | collective-permute-start | bytes 5308424 | tf_op jit(solution)/shard_map/ppermute | solution.py:284
  1214.1 116.1 %collective-permute-start.26 = (bf16[1,1536,576]{1,2,0:T(8,128)(2,1)}, bf16[1,1536,576]{1,2,0:T(8,128)(2,1)}, u32[]{:S(2)}, u32[]{:S(2)}) collective-permute-start(bf16[1,1536,576]{1,2,0:T(8,128)(2,1)} %copy.89), channel_id=1, source_target_pairs={{0,2},{1,3},{4,6},{5,7}} | collective-permute-start | bytes 5308424 | tf_op jit(solution)/shard_map/ppermute | solution.py:284
  1329.6 138.7 %collective-permute-start.24 = (bf16[1,1536,2048]{2,1,0:T(8,128)(2,1)}, bf16[1,1536,2048]{2,1,0:T(8,128)(2,1)}, u32[]{:S(2)}, u32[]{:S(2)}) collective-permute-start(bf16[1,1536,2048]{2,1,0:T(8,128)(2,1)} %collective-permute-done.20), channel_id=1, source_target_pairs={{0,4},{4,0},{1,5},{5,1},{2,6},{6,2},{3,7},{7,3}} | collective-permute-start | bytes 18874376 | tf_op jit(solution)/shard_map/ppermute | solution.py:298
  1337.6 260.0 %collective-permute-start.25 = (bf16[1,1536,2048]{2,1,0:T(8,128)(2,1)}, bf16[1,1536,2048]{2,1,0:T(8,128)(2,1)}, u32[]{:S(2)}, u32[]{:S(2)}) collective-permute-start(bf16[1,1536,2048]{2,1,0:T(8,128)(2,1)} %collective-permute-done.22), channel_id=1, source_target_pairs={{0,4},{4,0},{1,5},{5,1},{2,6},{6,2},{3,7},{7,3}} | collective-permute-start | bytes 18874376 | tf_op jit(solution)/shard_map/ppermute | solution.py:298

commit v2 on v1

--- a/solution.py
+++ b/solution.py
@@ -34,7 +34,7 @@
     return jnp.tile(cos_tab, (1, 2 * reps)), jnp.tile(jnp.concatenate([-sin_tab, sin_tab], axis=1), (1, reps))
 
 
-def attend_kernel(n_ret, aliased, ids, flags, hid, recv, w_dkv, gain, wq_own, wq_oth, kvo_own, kvo_oth, cos_ref, sin_ref, *rest):
+def attend_kernel(n_ret, aliased, ids, flags, hid, recv, w_dkv, gain, wq_own, wq_oth, kv_own, kv_oth, wo_own, wo_oth, cos_ref, sin_ref, *rest):
     if aliased:
         rest = rest[1:]
     if n_ret:
@@ -46,7 +46,7 @@
     req, blk = pl.program_id(0), pl.program_id(1)
     n_blocks = k_s.shape[0] // BLOCK
     kv_rank = gain.shape[1]
-    half = kvo_own.shape[1] // 2
+    half = wo_own.shape[0]
     n_heads = k_s.shape[1] // NOPE_DIM
     is_far = flags[0] == 1
     active = flags[1 + req] == 1
@@ -82,10 +82,10 @@
         kr_s[rows, :] = k_rope
         lat_ref[0, :, :kv_rank] = c_kv
         lat_ref[0, :, kv_rank:] = k_rope[:, :ROPE_DIM]
-        for idx, (wq, kvo) in enumerate(((wq_own, kvo_own), (wq_oth, kvo_oth))):
+        for idx, (wq, kv) in enumerate(((wq_own, kv_own), (wq_oth, kv_oth))):
             cols = slice(idx * half, (idx + 1) * half)
-            k_s[rows, cols] = jnp.dot(c_kv, kvo[:kv_rank, :half], preferred_element_type=jnp.float32).astype(jnp.bfloat16)
-            v_s[rows, cols] = jnp.dot(c_kv, kvo[:kv_rank, half:], preferred_element_type=jnp.float32).astype(jnp.bfloat16)
+            k_s[rows, cols] = jnp.dot(c_kv, kv[:, :half], preferred_element_type=jnp.float32).astype(jnp.bfloat16)
+            v_s[rows, cols] = jnp.dot(c_kv, kv[:, half:], preferred_element_type=jnp.float32).astype(jnp.bfloat16)
             q_s[:, cols] = jnp.dot(x_s[...], wq[:, :half], preferred_element_type=jnp.float32).astype(jnp.bfloat16)
             q_rope = jnp.dot(x_s[...], wq[:, half:], preferred_element_type=jnp.float32).astype(jnp.bfloat16)
             qr_s[:, idx * half // 2:(idx + 1) * half // 2] = rope(q_rope)
@@ -123,22 +123,22 @@
                     mixed = jnp.dot(src[:, :length], v_s[:length, cols], preferred_element_type=jnp.float32)
                     o_s[:, cols] = (mixed / total_ref[...]).astype(jnp.bfloat16)
 
-                def pair(idx, carry):
-                    head = idx * 2
-                    score(head + 1, 1, s1_s)
-                    weigh(s0_s, p0_s, t0_s)
-                    mix(jnp.maximum(head - 1, 0), p1_s, t1_s)
-                    score(jnp.minimum(head + 2, n_heads - 2), 0, s0_s)
-                    weigh(s1_s, p1_s, t1_s)
-                    mix(head, p0_s, t0_s)
+                def quad(idx, carry):
+                    for head in (idx * 4, idx * 4 + 2):
+                        score(head + 1, 1, s1_s)
+                        weigh(s0_s, p0_s, t0_s)
+                        mix(jnp.maximum(head - 1, 0), p1_s, t1_s)
+                        score(jnp.minimum(head + 2, n_heads - 2), 0, s0_s)
+                        weigh(s1_s, p1_s, t1_s)
+                        mix(head, p0_s, t0_s)
                     return carry
 
                 score(0, 0, s0_s)
-                lax.fori_loop(0, n_heads // 2, pair, 0)
+                lax.fori_loop(0, n_heads // 4, quad, 0)
                 mix(n_heads - 1, p1_s, t1_s)
 
-        y = jnp.dot(o_s[:, :half], kvo_own[kv_rank:, :], preferred_element_type=jnp.float32)
-        y = y + jnp.dot(o_s[:, half:], kvo_oth[kv_rank:, :], preferred_element_type=jnp.float32)
+        y = jnp.dot(o_s[:, :half], wo_own[...], preferred_element_type=jnp.float32)
+        y = y + jnp.dot(o_s[:, half:], wo_oth[...], preferred_element_type=jnp.float32)
         y = y.astype(jnp.bfloat16)
         if ret_ref is not None:
             @pl.when(req < n_ret)
@@ -157,16 +157,16 @@
 def attend(ids, flags, hidden, recv, weights, out_prev, n_ret):
     n_req = ids.shape[0]
     _, seq_len, width = hidden.shape
-    w_dkv, gain, wq_own, wq_oth, kvo_own, kvo_oth, _, _ = weights
+    w_dkv, gain, wq_own, wq_oth, kv_own, kv_oth, wo_own, wo_oth, _, _ = weights
     n_blocks = seq_len // BLOCK
     kv_rank = gain.shape[1]
-    half = kvo_own.shape[1] // 2
+    half = wo_own.shape[0]
     lat_width = kv_rank + ROPE_DIM
     whole = lambda arr: pl.BlockSpec(arr.shape, lambda r, i, ids, flags: (0, 0), pipeline_mode=pl.Buffered(1))
     in_specs = [
         pl.BlockSpec((1, BLOCK, width), lambda r, i, ids, flags: (jnp.where(flags[0] == 1, 0, ids[r]), jnp.where(flags[0] == 1, 0, i), 0)),
         pl.BlockSpec((1, BLOCK, width), lambda r, i, ids, flags: (0, jnp.where((flags[0] == 1) & (r == 0), i, 0), 0)),
-        *[whole(arr) for arr in (w_dkv, gain, wq_own, wq_oth, kvo_own, kvo_oth)],
+        *[whole(arr) for arr in (w_dkv, gain, wq_own, wq_oth, kv_own, kv_oth, wo_own, wo_oth)],
         pl.BlockSpec((BLOCK, LANES), lambda r, i, ids, flags: (i, 0)),
         pl.BlockSpec((BLOCK, LANES), lambda r, i, ids, flags: (i, 0)),
     ]
@@ -246,20 +246,22 @@
         arrivals = []
         for idx in range(N_FAR):
             index = own + idx
+            if idx > 1:
+                index, _ = lax.optimization_barrier((index, arrivals[-2]))
+            piece = lax.dynamic_slice_in_dim(tokens, index, 1, axis=0)
             if arrivals:
-                index, _ = lax.optimization_barrier((index, arrivals[-1]))
-            piece = lax.dynamic_slice_in_dim(tokens, index, 1, axis=0)
+                piece, _ = lax.optimization_barrier((piece, arrivals[-1]))
             arrivals.append(lax.ppermute(piece, "stage", down))
 
         heads_here = w_uk.shape[1] // NOPE_DIM
         wq = w_query.reshape(width, heads_here, NOPE_DIM + ROPE_DIM)
         wq_own = jnp.concatenate([wq[:, :, :NOPE_DIM].reshape(width, -1), wq[:, :, NOPE_DIM:].reshape(width, -1)], axis=1)
-        kvo_own = jnp.concatenate([jnp.concatenate([w_uk, w_uv], axis=1), w_out], axis=0)
-        wq_oth, kvo_oth = other_half(wq_own, core), other_half(kvo_own, core)
+        kv_own = jnp.concatenate([w_uk, w_uv], axis=1)
+        wo_oth, kv_oth, wq_oth = other_half(w_out, core), other_half(kv_own, core), other_half(wq_own, core)
         blank = jnp.zeros((width, ROPE_DIM), w_dkv.dtype)
         w_dkv_wide = jnp.concatenate([w_dkv, blank, blank, w_dkv[:, kv_rank:]], axis=1)
         gain = latent_gain.astype(jnp.float32)[None, :]
-        weights = (w_dkv_wide, gain, wq_own, wq_oth, kvo_own, kvo_oth, *rope_tables(seq_len))
+        weights = (w_dkv_wide, gain, wq_own, wq_oth, kv_own, kv_oth, w_out, wo_oth, *rope_tables(seq_len))
 
         ids = jnp.concatenate([own + jnp.arange(N_FAR, n_half), oth + jnp.arange(N_FAR + N_SWAP, n_half)]).astype(jnp.int32)
         far = jnp.where(is_prompt, 0, 1).astype(jnp.int32)

time: 1620 us -> 1590 us (0.981)
    dynamic_slice x7 -> x4, local copies, waits for them, and re-layouts: 46.4 us -> 43 us  [device_step(): piece = lax.dynamic_slice_in_dim(tokens, index, 1, axis=0)]
    ppermute x2 -> x3, waiting for transfers between devices: 93.6 us -> 94.9 us  [other_half(): lax.ppermute(lax.dynamic_slice_in_dim(arr, core * rows, rows, axis=0), 't...]
  transfers between devices with their start and end apart: 31 -> 33, of which waited for: 8 -> 9; matrix products, arithmetic and copies ran while one was open for 16% -> 14% of each run, Pallas kernels for 63% -> 63%
where the time goes in v2:
time: 1590 us
  Pallas kernels  1010 us (64%)
  waiting for transfers between devices  236 us (15%)
  other arithmetic  148 us (9%)
  local copies, waits for them, and re-layouts  110 us (7%)
  starting transfers between devices  84 us (5%)
    pallas_call x9, Pallas kernels, attend(): pl.pallas_call(functools.partial(attend_kernel, n_ret, out_prev is not No...  1010 us
    ppermute x7, waiting for transfers between devices, device_step(): moved = lax.ppermute(back, 't', swap)  126 us
    dynamic_update_slice x15, other arithmetic, device_step(): lax.dynamic_update_slice(out, jnp.where(is_prompt, block, jnp.zeros_like(...  116 us
    ppermute x3, waiting for transfers between devices, other_half(): lax.ppermute(lax.dynamic_slice_in_dim(arr, core * rows, rows, axis=0), 't...  94.9 us
    dynamic_slice x4, local copies, waits for them, and re-layouts, device_step(): piece = lax.dynamic_slice_in_dim(tokens, index, 1, axis=0)  43 us
    ppermute x7, starting transfers between devices, device_step(): arrivals.append(lax.ppermute(piece, 'stage', down))  41.9 us
  transfers between devices with their start and end apart: 33, of which 9 were waited for; matrix products, arithmetic and copies ran while one was open for 14% of the time, Pallas kernels for 63%

profile of v2, /device:TPU:0, one launch (start us, length us, event | category | flops | bytes accessed | tf_op | source)
XLA Modules:
  0.0 1585.7 jit_solution(4143004911134529307)
XLA Ops:
  0.6 8.6 copy.68
  9.3 4.8 slice.49
  17.2 6.4 copy.101
  33.4 12.2 dynamic-slice_bitcast_fusion.4
  45.6 6.0 collective-permute-start.6
  63.7 39.1 %collective-permute-done = bf16[1024,1536]{1,0:T(8,128)(2,1)} collective-permute-done((bf16[1024,1536]{1,0:T(8,128)(2,1)}, bf16[1024,1536]{1,0:T(8,128)(2,1)}, u32[]{:S(2)}, u32[]{:S(2)}) %collective-permute-start) | collective-permute-done | bytes 3145760 | tf_op jit(solution)/shard_map/ppermute | solution.py:229
  104.6 4.3 copy.67
  112.9 34.8 %collective-permute-done.4 = bf16[512,2048]{1,0:T(8,128)(2,1)} collective-permute-done((bf16[512,2048]{1,0:T(8,128)(2,1)}, bf16[512,2048]{1,0:T(8,128)(2,1)}, u32[]{:S(2)}, u32[]{:S(2)}) %collective-permute-start.4) | collective-permute-done | bytes 2097184 | tf_op jit(solution)/shard_map/ppermute | solution.py:229
  148.2 21.0 %collective-permute-done.2 = bf16[256,2048]{1,0:T(8,128)(2,1)} collective-permute-done((bf16[256,2048]{1,0:T(8,128)(2,1)}, bf16[256,2048]{1,0:T(8,128)(2,1)}, u32[]{:S(2)}, u32[]{:S(2)}) %collective-permute-start.2) | collective-permute-done | bytes 1048608 | tf_op jit(solution)/shard_map/ppermute | solution.py:229
  184.4 6.6 collective-permute-start.7
  190.9 4.9 broadcast_select_fusion.1
  195.9 5.0 pad_maximum_fusion.1.wq_oth
  200.8 108.5 %attend.9 = (bf16[24,1536,2048]{2,1,0:T(8,128)(2,1)}, bf16[1,1536,576]{2,1,0:T(8,128)(2,1)}, bf16[1,1536,2048]{2,1,0:T(8,128)(2,1)}) custom-call(s32[1]{0:T(128)} %get-tuple-element.167.ids, s32[2]{0:T(128)} %pad_add_fusion.1.flags, bf16[24,1536,2048]{2,1,0:T(8,128)(2,1)} %bitcast.3.hid.recv, bf16[1,1536,2048]{2,1,0:T(8,128)(2,1)} %collective-permute-done.6.recv, ...), custom_call_target="tpu_custom_call" | custom-call | flops 57982058496 | bytes 18874368 | tf_op jit(solution)/shard_map/attend/pallas_call | solution.py:188
  312.0 11.8 collective-permute-done.7.recv
  323.7 12.0 dynamic-slice_bitcast_fusion.2
  335.8 7.0 collective-permute-start.8
  342.8 122.8 %attend.10 = (bf16[24,1536,2048]{2,1,0:T(8,128)(2,1)}, bf16[1,1536,576]{2,1,0:T(8,128)(2,1)}, bf16[1,1536,2048]{2,1,0:T(8,128)(2,1)}) custom-call(s32[1]{0:T(128)} %get-tuple-element.168.ids, s32[2]{0:T(128)} %pad_add_fusion.1.flags, bf16[24,1536,2048]{2,1,0:T(8,128)(2,1)} %bitcast.3.hid.recv, ...), custom_call_target="tpu_custom_call", output_to_operand_aliasing={{0}: (14, {})} | custom-call | flops 57982058496 | bytes 18874368 | tf_op jit(solution)/shard_map/attend/pallas_call | solution.py:188
  468.4 7.7 select_dynamic-update-slice_fusion.12.rest_0_
  476.2 7.0 collective-permute-start.9
  483.2 122.0 %attend.11 = (bf16[24,1536,2048]{2,1,0:T(8,128)(2,1)}, bf16[1,1536,576]{2,1,0:T(8,128)(2,1)}, bf16[1,1536,2048]{2,1,0:T(8,128)(2,1)}) custom-call(s32[1]{0:T(128)} %get-tuple-element.169.ids, s32[2]{0:T(128)} %pad_add_fusion.1.flags, bf16[24,1536,2048]{2,1,0:T(8,128)(2,1)} %bitcast.3.hid.recv, ...), custom_call_target="tpu_custom_call", output_to_operand_aliasing={{0}: (14, {})} | custom-call | flops 57982058496 | bytes 18874368 | tf_op jit(solution)/shard_map/attend/pallas_call | solution.py:188
  607.0 7.7 select_dynamic-update-slice_fusion.11.rest_0_
  614.7 12.1 dynamic-slice_bitcast_fusion
  626.8 7.1 collective-permute-start.10
  633.9 108.9 %attend.12 = (bf16[24,1536,2048]{2,1,0:T(8,128)(2,1)}, bf16[1,1536,576]{2,1,0:T(8,128)(2,1)}, bf16[1,1536,2048]{2,1,0:T(8,128)(2,1)}) custom-call(s32[1]{0:T(128)} %get-tuple-element.170.ids, s32[2]{0:T(128)} %pad_add_fusion.1.flags, bf16[24,1536,2048]{2,1,0:T(8,128)(2,1)} %bitcast.3.hid.recv, ...), custom_call_target="tpu_custom_call", output_to_operand_aliasing={{0}: (14, {})} | custom-call | flops 57982058496 | bytes 18874368 | tf_op jit(solution)/shard_map/attend/pallas_call | solution.py:188
  744.6 7.7 select_dynamic-update-slice_fusion.10
  753.4 7.7 select_dynamic-update-slice_fusion.9
  761.1 7.7 select_dynamic-update-slice_fusion.8.rest_0_
  772.7 108.9 %attend.13 = (bf16[24,1536,2048]{2,1,0:T(8,128)(2,1)}, bf16[1,1536,576]{2,1,0:T(8,128)(2,1)}, bf16[1,1536,2048]{2,1,0:T(8,128)(2,1)}) custom-call(s32[1]{0:T(128)} %get-tuple-element.171.ids, s32[2]{0:T(128)} %pad_add_fusion.1.flags, bf16[24,1536,2048]{2,1,0:T(8,128)(2,1)} %bitcast.3.hid.recv, ...), custom_call_target="tpu_custom_call", output_to_operand_aliasing={{0}: (14, {})} | custom-call | flops 57982058496 | bytes 18874368 | tf_op jit(solution)/shard_map/attend/pallas_call | solution.py:188
  883.9 7.7 select_dynamic-update-slice_fusion.7
  891.7 7.7 select_dynamic-update-slice_fusion.6.rest_0_
  899.3 6.6 dynamic-slice_bitcast_fusion.1
  910.2 108.9 %attend.14 = (bf16[24,1536,2048]{2,1,0:T(8,128)(2,1)}, bf16[1,1536,576]{2,1,0:T(8,128)(2,1)}, bf16[1,1536,2048]{2,1,0:T(8,128)(2,1)}) custom-call(s32[1]{0:T(128)} %get-tuple-element.172.ids, s32[2]{0:T(128)} %pad_add_fusion.1.flags, bf16[24,1536,2048]{2,1,0:T(8,128)(2,1)} %bitcast.3.hid.recv, ...), custom_call_target="tpu_custom_call", output_to_operand_aliasing={{0}: (14, {})} | custom-call | flops 57982058496 | bytes 18874368 | tf_op jit(solution)/shard_map/attend/pallas_call | solution.py:188
  1021.6 7.7 select_dynamic-update-slice_fusion.5
  1029.3 7.7 select_dynamic-update-slice_fusion.4.rest_0_
  1043.8 5.6 collective-permute-start.32
  1058.2 108.9 %attend.15 = (bf16[24,1536,2048]{2,1,0:T(8,128)(2,1)}, bf16[1,1536,576]{2,1,0:T(8,128)(2,1)}, bf16[1,1536,2048]{2,1,0:T(8,128)(2,1)}) custom-call(s32[1]{0:T(128)} %get-tuple-element.173.ids, s32[2]{0:T(128)} %pad_add_fusion.1.flags, bf16[24,1536,2048]{2,1,0:T(8,128)(2,1)} %bitcast.3.hid.recv, ...), custom_call_target="tpu_custom_call", output_to_operand_aliasing={{0}: (14, {})} | custom-call | flops 57982058496 | bytes 18874368 | tf_op jit(solution)/shard_map/attend/pallas_call | solution.py:188
  1169.6 7.8 select_dynamic-update-slice_fusion.3
  1185.0 7.7 select_dynamic-update-slice_fusion.2.rest_0_
  1192.7 5.7 collective-permute-start.29
  1201.0 108.8 %attend.16 = (bf16[24,1536,2048]{2,1,0:T(8,128)(2,1)}, bf16[1,1536,576]{2,1,0:T(8,128)(2,1)}) custom-call(s32[1]{0:T(128)} %get-tuple-element.174.ids, s32[2]{0:T(128)} %pad_add_fusion.flags, bf16[24,1536,2048]{2,1,0:T(8,128)(2,1)} %bitcast.3.hid.recv, bf16[24,1536,2048]{2,1,0:T(8,128)(2,1)} %bitcast.3.hid.recv, ...), custom_call_target="tpu_custom_call", output_to_operand_aliasing={{0}: (14, {})} | custom-call | flops 57982058496 | bytes 18874368 | tf_op jit(solution)/shard_map/attend/pallas_call | solution.py:188
  1311.0 7.4 conditional.1
  1311.0 7.4 broadcast.37
  1320.4 7.7 select_dynamic-update-slice_fusion.1
  1328.1 7.7 select_dynamic-update-slice_fusion.rest_0_
  1335.8 108.7 %attend.17 = (bf16[24,1536,2048]{2,1,0:T(8,128)(2,1)}, bf16[1,1536,576]{2,1,0:T(8,128)(2,1)}) custom-call(s32[1]{0:T(128)} %get-tuple-element.175.ids, s32[2]{0:T(128)} %pad_add_fusion.flags, bf16[24,1536,2048]{2,1,0:T(8,128)(2,1)} %bitcast.3.hid.recv, bf16[24,1536,2048]{2,1,0:T(8,128)(2,1)} %bitcast.3.hid.recv, ...), custom_call_target="tpu_custom_call", output_to_operand_aliasing={{0}: (14, {})} | custom-call | flops 57982058496 | bytes 18874368 | tf_op jit(solution)/shard_map/attend/pallas_call | solution.py:188
  1448.6 7.7 bitcast_dynamic-update-slice_fusion.1
  1456.2 121.6 %collective-permute-done.27 = bf16[1,1536,2048]{2,1,0:T(8,128)(2,1)} collective-permute-done((bf16[1,1536,2048]{2,1,0:T(8,128)(2,1)}, bf16[1,1536,2048]{2,1,0:T(8,128)(2,1)}, u32[]{:S(2)}, u32[]{:S(2)}) %collective-permute-start.27) | collective-permute-done | bytes 6291488 | tf_op jit(solution)/shard_map/ppermute | solution.py:300
  1577.8 7.7 bitcast_dynamic-update-slice_fusion
  (101 shorter events, 104.8 us)
Async XLA Ops:
  30.1 72.6 %collective-permute-start = (bf16[1024,1536]{1,0:T(8,128)(2,1)}, bf16[1024,1536]{1,0:T(8,128)(2,1)}, u32[]{:S(2)}, u32[]{:S(2)}) collective-permute-start(bf16[1024,1536]{1,0:T(8,128)(2,1)} %fusion), channel_id=1, source_target_pairs={{0,4},{4,0},{1,5},{5,1},{2,6},{6,2},{3,7},{7,3}} | collective-permute-start | bytes 9437192 | tf_op jit(solution)/shard_map/ppermute | solution.py:229
  33.4 21.9 %copy-start.6 = (bf16[512,1024]{1,0:T(8,128)(2,1)S(1)}, bf16[512,1024]{1,0:T(8,128)(2,1)}, u32[]{:S(2)}) copy-start(bf16[512,1024]{1,0:T(8,128)(2,1)} %param.13) | copy-start | bytes 3145732
  45.6 138.7 %collective-permute-start.6 = (bf16[1,1536,2048]{2,1,0:T(8,128)(2,1)}, bf16[1,1536,2048]{2,1,0:T(8,128)(2,1)}, u32[]{:S(2)}, u32[]{:S(2)}) collective-permute-start(bf16[1,1536,2048]{2,1,0:T(8,128)(2,1)} %get-tuple-element.160), channel_id=1, source_target_pairs={{0,2},{1,3},{4,6},{5,7}} | collective-permute-start | bytes 18874376 | tf_op jit(solution)/shard_map/ppermute | solution.py:254
  54.8 92.8 %collective-permute-start.4 = (bf16[512,2048]{1,0:T(8,128)(2,1)}, bf16[512,2048]{1,0:T(8,128)(2,1)}, u32[]{:S(2)}, u32[]{:S(2)}) collective-permute-start(bf16[512,2048]{1,0:T(8,128)(2,1)} %constant_dynamic-slice_fusion), channel_id=1, source_target_pairs={{0,4},{4,0},{1,5},{5,1},{2,6},{6,2},{3,7},{7,3}} | collective-permute-start | bytes 6291464 | tf_op jit(solution)/shard_map/ppermute | solution.py:229
  56.8 1.4 copy-start
  59.3 110.0 %collective-permute-start.2 = (bf16[256,2048]{1,0:T(8,128)(2,1)}, bf16[256,2048]{1,0:T(8,128)(2,1)}, u32[]{:S(2)}, u32[]{:S(2)}) collective-permute-start(bf16[256,2048]{1,0:T(8,128)(2,1)} %constant_dynamic-slice_fusion.1), channel_id=1, source_target_pairs={{0,4},{4,0},{1,5},{5,1},{2,6},{6,2},{3,7},{7,3}} | collective-permute-start | bytes 3145736 | tf_op jit(solution)/shard_map/ppermute | solution.py:229
  62.1 50.1 %copy-start.7 = (bf16[512]{0:T(512)(128)(2,1)S(1)}, bf16[512]{0:T(512)(128)(2,1)}, u32[]{:S(2)}) copy-start(bf16[512]{0:T(512)(128)(2,1)} %param.12) | copy-start | bytes 3076
  102.7 88.2 %collective-permute-start.1 = (bf16[1024,1536]{1,0:T(8,128)(2,1)}, bf16[1024,1536]{1,0:T(8,128)(2,1)}, u32[]{:S(2)}, u32[]{:S(2)}) collective-permute-start(bf16[1024,1536]{1,0:T(8,128)(2,1)} %collective-permute-done), channel_id=1, source_target_pairs={{0,1},{1,0},{2,3},{3,2},{4,5},{5,4},{6,7},{7,6}} | collective-permute-start | bytes 9437192 | tf_op jit(solution)/shard_map/ppermute | solution.py:230
  112.9 60.6 %copy-start.1 = (bf16[2048,1024]{1,0:T(8,128)(2,1)S(1)}, bf16[2048,1024]{1,0:T(8,128)(2,1)}, u32[]{:S(2)}) copy-start(bf16[2048,1024]{1,0:T(8,128)(2,1)} %copy.101) | copy-start | bytes 12582916
  147.6 32.3 %collective-permute-start.5 = (bf16[512,2048]{1,0:T(8,128)(2,1)}, bf16[512,2048]{1,0:T(8,128)(2,1)S(1)}, u32[]{:S(2)}, u32[]{:S(2)}) collective-permute-start(bf16[512,2048]{1,0:T(8,128)(2,1)} %collective-permute-done.4), channel_id=1, source_target_pairs={{0,1},{1,0},{2,3},{3,2},{4,5},{5,4},{6,7},{7,6}} | collective-permute-start | bytes 6291464 | tf_op jit(solution)/shard_map/ppermute | solution.py:230
  169.3 7.4 collective-permute-start.3
  184.4 139.4 %collective-permute-start.7 = (bf16[1,1536,2048]{2,1,0:T(8,128)(2,1)}, bf16[1,1536,2048]{2,1,0:T(8,128)(2,1)}, u32[]{:S(2)}, u32[]{:S(2)}) collective-permute-start(bf16[1,1536,2048]{2,1,0:T(8,128)(2,1)} %get-tuple-element.81), channel_id=1, source_target_pairs={{0,2},{1,3},{4,6},{5,7}} | collective-permute-start | bytes 18874376 | tf_op jit(solution)/shard_map/ppermute | solution.py:254
  309.4 157.5 %collective-permute-start.13 = (bf16[1,1536,2048]{2,1,0:T(8,128)(2,1)}, bf16[1,1536,2048]{2,1,0:T(8,128)(2,1)}, u32[]{:S(2)}, u32[]{:S(2)}) collective-permute-start(bf16[1,1536,2048]{2,1,0:T(8,128)(2,1)} %get-tuple-element.93), channel_id=1, source_target_pairs={{2,0},{3,1},{6,4},{7,5}} | collective-permute-start | bytes 18874376 | tf_op jit(solution)/shard_map/ppermute | solution.py:299
  310.7 450.4 %collective-permute-start.17 = (bf16[1,1536,2048]{2,1,0:T(8,128)(2,1)}, bf16[1,1536,2048]{2,1,0:T(8,128)(2,1)}, u32[]{:S(2)}, u32[]{:S(2)}) collective-permute-start(bf16[1,1536,2048]{2,1,0:T(8,128)(2,1)} %get-tuple-element.93), channel_id=1, source_target_pairs={{0,4},{4,0},{1,5},{5,1},{2,6},{6,2},{3,7},{7,3}} | collective-permute-start | bytes 18874376 | tf_op jit(solution)/shard_map/ppermute | solution.py:298
  335.8 140.4 %collective-permute-start.8 = (bf16[1,1536,2048]{2,1,0:T(8,128)(2,1)}, bf16[1,1536,2048]{2,1,0:T(8,128)(2,1)}, u32[]{:S(2)}, u32[]{:S(2)}) collective-permute-start(bf16[1,1536,2048]{2,1,0:T(8,128)(2,1)} %get-tuple-element.82), channel_id=1, source_target_pairs={{0,2},{1,3},{4,6},{5,7}} | collective-permute-start | bytes 18874376 | tf_op jit(solution)/shard_map/ppermute | solution.py:254
  465.6 140.9 %collective-permute-start.14 = (bf16[1,1536,2048]{2,1,0:T(8,128)(2,1)}, bf16[1,1536,2048]{2,1,0:T(8,128)(2,1)}, u32[]{:S(2)}, u32[]{:S(2)}) collective-permute-start(bf16[1,1536,2048]{2,1,0:T(8,128)(2,1)} %get-tuple-element.95), channel_id=1, source_target_pairs={{2,0},{3,1},{6,4},{7,5}} | collective-permute-start | bytes 18874376 | tf_op jit(solution)/shard_map/ppermute | solution.py:299
  466.9 285.4 %collective-permute-start.16 = (bf16[1,1536,2048]{2,1,0:T(8,128)(2,1)}, bf16[1,1536,2048]{2,1,0:T(8,128)(2,1)}, u32[]{:S(2)}, u32[]{:S(2)}) collective-permute-start(bf16[1,1536,2048]{2,1,0:T(8,128)(2,1)} %collective-permute-done.13), channel_id=1, source_target_pairs={{0,4},{4,0},{1,5},{5,1},{2,6},{6,2},{3,7},{7,3}} | collective-permute-start | bytes 18874376 | tf_op jit(solution)/shard_map/ppermute | solution.py:300
  476.2 138.6 %collective-permute-start.9 = (bf16[1,1536,2048]{2,1,0:T(8,128)(2,1)}, bf16[1,1536,2048]{2,1,0:T(8,128)(2,1)}, u32[]{:S(2)}, u32[]{:S(2)}) collective-permute-start(bf16[1,1536,2048]{2,1,0:T(8,128)(2,1)} %get-tuple-element.85), channel_id=1, source_target_pairs={{0,2},{1,3},{4,6},{5,7}} | collective-permute-start | bytes 18874376 | tf_op jit(solution)/shard_map/ppermute | solution.py:254
  605.2 138.2 %collective-permute-start.15 = (bf16[1,1536,2048]{2,1,0:T(8,128)(2,1)}, bf16[1,1536,2048]{2,1,0:T(8,128)(2,1)}, u32[]{:S(2)}, u32[]{:S(2)}) collective-permute-start(bf16[1,1536,2048]{2,1,0:T(8,128)(2,1)} %get-tuple-element.97), channel_id=1, source_target_pairs={{2,0},{3,1},{6,4},{7,5}} | collective-permute-start | bytes 18874376 | tf_op jit(solution)/shard_map/ppermute | solution.py:299
  606.5 285.2 %collective-permute-start.19 = (bf16[1,1536,2048]{2,1,0:T(8,128)(2,1)}, bf16[1,1536,2048]{2,1,0:T(8,128)(2,1)}, u32[]{:S(2)}, u32[]{:S(2)}) collective-permute-start(bf16[1,1536,2048]{2,1,0:T(8,128)(2,1)} %collective-permute-done.14), channel_id=1, source_target_pairs={{0,4},{4,0},{1,5},{5,1},{2,6},{6,2},{3,7},{7,3}} | collective-permute-start | bytes 18874376 | tf_op jit(solution)/shard_map/ppermute | solution.py:300
  626.8 141.9 %collective-permute-start.10 = (bf16[1,1536,2048]{2,1,0:T(8,128)(2,1)}, bf16[1,1536,2048]{2,1,0:T(8,128)(2,1)}, u32[]{:S(2)}, u32[]{:S(2)}) collective-permute-start(bf16[1,1536,2048]{2,1,0:T(8,128)(2,1)} %get-tuple-element.86), channel_id=1, source_target_pairs={{0,2},{1,3},{4,6},{5,7}} | collective-permute-start | bytes 18874376 | tf_op jit(solution)/shard_map/ppermute | solution.py:254
  743.3 139.7 %collective-permute-start.18 = (bf16[1,1536,2048]{2,1,0:T(8,128)(2,1)}, bf16[1,1536,2048]{2,1,0:T(8,128)(2,1)}, u32[]{:S(2)}, u32[]{:S(2)}) collective-permute-start(bf16[1,1536,2048]{2,1,0:T(8,128)(2,1)} %get-tuple-element.99), channel_id=1, source_target_pairs={{2,0},{3,1},{6,4},{7,5}} | collective-permute-start | bytes 18874376 | tf_op jit(solution)/shard_map/ppermute | solution.py:299
  752.3 277.0 %collective-permute-start.21 = (bf16[1,1536,2048]{2,1,0:T(8,128)(2,1)}, bf16[1,1536,2048]{2,1,0:T(8,128)(2,1)}, u32[]{:S(2)}, u32[]{:S(2)}) collective-permute-start(bf16[1,1536,2048]{2,1,0:T(8,128)(2,1)} %collective-permute-done.15), channel_id=1, source_target_pairs={{0,4},{4,0},{1,5},{5,1},{2,6},{6,2},{3,7},{7,3}} | collective-permute-start | bytes 18874376 | tf_op jit(solution)/shard_map/ppermute | solution.py:300
  768.8 137.2 %collective-permute-start.11 = (bf16[1,1536,2048]{2,1,0:T(8,128)(2,1)}, bf16[1,1536,2048]{2,1,0:T(8,128)(2,1)}, u32[]{:S(2)}, u32[]{:S(2)}) collective-permute-start(bf16[1,1536,2048]{2,1,0:T(8,128)(2,1)} %get-tuple-element.89), channel_id=1, source_target_pairs={{0,2},{1,3},{4,6},{5,7}} | collective-permute-start | bytes 18874376 | tf_op jit(solution)/shard_map/ppermute | solution.py:254
  881.7 138.8 %collective-permute-start.20 = (bf16[1,1536,2048]{2,1,0:T(8,128)(2,1)}, bf16[1,1536,2048]{2,1,0:T(8,128)(2,1)}, u32[]{:S(2)}, u32[]{:S(2)}) collective-permute-start(bf16[1,1536,2048]{2,1,0:T(8,128)(2,1)} %get-tuple-element.101), channel_id=1, source_target_pairs={{2,0},{3,1},{6,4},{7,5}} | collective-permute-start | bytes 18874376 | tf_op jit(solution)/shard_map/ppermute | solution.py:299
  883.0 300.7 %collective-permute-start.23 = (bf16[1,1536,2048]{2,1,0:T(8,128)(2,1)}, bf16[1,1536,2048]{2,1,0:T(8,128)(2,1)}, u32[]{:S(2)}, u32[]{:S(2)}) collective-permute-start(bf16[1,1536,2048]{2,1,0:T(8,128)(2,1)} %collective-permute-done.18), channel_id=1, source_target_pairs={{0,4},{4,0},{1,5},{5,1},{2,6},{6,2},{3,7},{7,3}} | collective-permute-start | bytes 18874376 | tf_op jit(solution)/shard_map/ppermute | solution.py:300
  906.0 133.9 %collective-permute-start.12 = (bf16[1,1536,2048]{2,1,0:T(8,128)(2,1)}, bf16[1,1536,2048]{2,1,0:T(8,128)(2,1)}, u32[]{:S(2)}, u32[]{:S(2)}) collective-permute-start(bf16[1,1536,2048]{2,1,0:T(8,128)(2,1)} %dynamic-slice_bitcast_fusion.1), channel_id=1, source_target_pairs={{0,2},{1,3},{4,6},{5,7}} | collective-permute-start | bytes 18874376 | tf_op jit(solution)/shard_map/ppermute | solution.py:254
  1019.2 147.9 %collective-permute-start.22 = (bf16[1,1536,2048]{2,1,0:T(8,128)(2,1)}, bf16[1,1536,2048]{2,1,0:T(8,128)(2,1)}, u32[]{:S(2)}, u32[]{:S(2)}) collective-permute-start(bf16[1,1536,2048]{2,1,0:T(8,128)(2,1)} %get-tuple-element.103), channel_id=1, source_target_pairs={{2,0},{3,1},{6,4},{7,5}} | collective-permute-start | bytes 18874376 | tf_op jit(solution)/shard_map/ppermute | solution.py:299
  1020.5 307.6 %collective-permute-start.25 = (bf16[1,1536,2048]{2,1,0:T(8,128)(2,1)}, bf16[1,1536,2048]{2,1,0:T(8,128)(2,1)}, u32[]{:S(2)}, u32[]{:S(2)}) collective-permute-start(bf16[1,1536,2048]{2,1,0:T(8,128)(2,1)} %collective-permute-done.20), channel_id=1, source_target_pairs={{0,4},{4,0},{1,5},{5,1},{2,6},{6,2},{3,7},{7,3}} | collective-permute-start | bytes 18874376 | tf_op jit(solution)/shard_map/ppermute | solution.py:300
  1037.0 18.9 %copy-start.4 = (bf16[1,1536,576]{2,1,0:T(8,128)(2,1)S(1)}, bf16[1,1536,576]{2,1,0:T(8,128)(2,1)}, u32[]{:S(2)}) copy-start(bf16[1,1536,576]{2,1,0:T(8,128)(2,1)} %get-tuple-element.116) | copy-start | bytes 5308420
  1043.8 148.8 %collective-permute-start.32 = (bf16[1,1536,576]{1,2,0:T(8,128)(2,1)}, bf16[1,1536,576]{1,2,0:T(8,128)(2,1)}, u32[]{:S(2)}, u32[]{:S(2)}) collective-permute-start(bf16[1,1536,576]{1,2,0:T(8,128)(2,1)} %copy.93), channel_id=1, source_target_pairs={{0,2},{1,3},{4,6},{5,7}} | collective-permute-start | bytes 5308424 | tf_op jit(solution)/shard_map/ppermute | solution.py:286
  1053.3 145.0 %collective-permute-start.31 = (bf16[1,1536,576]{1,2,0:T(8,128)(2,1)}, bf16[1,1536,576]{1,2,0:T(8,128)(2,1)}, u32[]{:S(2)}, u32[]{:S(2)}) collective-permute-start(bf16[1,1536,576]{1,2,0:T(8,128)(2,1)} %copy.92), channel_id=1, source_target_pairs={{0,2},{1,3},{4,6},{5,7}} | collective-permute-start | bytes 5308424 | tf_op jit(solution)/shard_map/ppermute | solution.py:286
  1167.1 142.7 %collective-permute-start.30 = (bf16[1,1536,576]{1,2,0:T(8,128)(2,1)}, bf16[1,1536,576]{1,2,0:T(8,128)(2,1)}, u32[]{:S(2)}, u32[]{:S(2)}) collective-permute-start(bf16[1,1536,576]{1,2,0:T(8,128)(2,1)} %copy.91), channel_id=1, source_target_pairs={{0,2},{1,3},{4,6},{5,7}} | collective-permute-start | bytes 5308424 | tf_op jit(solution)/shard_map/ppermute | solution.py:286
  1169.6 11.7 copy-start.2
  1183.7 135.6 %collective-permute-start.24 = (bf16[1,1536,2048]{2,1,0:T(8,128)(2,1)}, bf16[1,1536,2048]{2,1,0:T(8,128)(2,1)}, u32[]{:S(2)}, u32[]{:S(2)}) collective-permute-start(bf16[1,1536,2048]{2,1,0:T(8,128)(2,1)} %get-tuple-element.105), channel_id=1, source_target_pairs={{2,0},{3,1},{6,4},{7,5}} | collective-permute-start | bytes 18874376 | tf_op jit(solution)/shard_map/ppermute | solution.py:299
  1192.7 118.3 %collective-permute-start.29 = (bf16[1,1536,576]{1,2,0:T(8,128)(2,1)}, bf16[1,1536,576]{1,2,0:T(8,128)(2,1)}, u32[]{:S(2)}, u32[]{:S(2)}) collective-permute-start(bf16[1,1536,576]{1,2,0:T(8,128)(2,1)} %copy.90), channel_id=1, source_target_pairs={{0,2},{1,3},{4,6},{5,7}} | collective-permute-start | bytes 5308424 | tf_op jit(solution)/shard_map/ppermute | solution.py:286
  1198.4 112.6 %collective-permute-start.28 = (bf16[1,1536,576]{1,2,0:T(8,128)(2,1)}, bf16[1,1536,576]{1,2,0:T(8,128)(2,1)}, u32[]{:S(2)}, u32[]{:S(2)}) collective-permute-start(bf16[1,1536,576]{1,2,0:T(8,128)(2,1)} %copy.89), channel_id=1, source_target_pairs={{0,2},{1,3},{4,6},{5,7}} | collective-permute-start | bytes 5308424 | tf_op jit(solution)/shard_map/ppermute | solution.py:286
  1309.8 138.7 %collective-permute-start.26 = (bf16[1,1536,2048]{2,1,0:T(8,128)(2,1)}, bf16[1,1536,2048]{2,1,0:T(8,128)(2,1)}, u32[]{:S(2)}, u32[]{:S(2)}) collective-permute-start(bf16[1,1536,2048]{2,1,0:T(8,128)(2,1)} %collective-permute-done.22), channel_id=1, source_target_pairs={{0,4},{4,0},{1,5},{5,1},{2,6},{6,2},{3,7},{7,3}} | collective-permute-start | bytes 18874376 | tf_op jit(solution)/shard_map/ppermute | solution.py:300
  1319.3 258.6 %collective-permute-start.27 = (bf16[1,1536,2048]{2,1,0:T(8,128)(2,1)}, bf16[1,1536,2048]{2,1,0:T(8,128)(2,1)}, u32[]{:S(2)}, u32[]{:S(2)}) collective-permute-start(bf16[1,1536,2048]{2,1,0:T(8,128)(2,1)} %collective-permute-done.24), channel_id=1, source_target_pairs={{0,4},{4,0},{1,5},{5,1},{2,6},{6,2},{3,7},{7,3}} | collective-permute-start | bytes 18874376 | tf_op jit(solution)/shard_map/ppermute | solution.py:300
